TPU v7x, 64 devices: a 2x2x8 block of a 4x4x8 slice. The times are simulated.
64 devices in a mesh: dp: 4 (over x, y), sp: 16 (over z, core).
Axes of the slice: x: 2, y: 2, z: 8, core: 2. Of those that a mesh axis runs over, the one named last changes fastest.
The devices are a block of a 4x4x8 slice.
Arguments:
- hidden: bfloat16 [8192, 4096], P(('dp', 'sp')), parts along dimension 0
- ln_gain: bfloat16 [4096], replicated
- w_q: bfloat16 [4096, 4096], replicated
- w_k: bfloat16 [4096, 1024], replicated
- w_v: bfloat16 [4096, 1024], replicated
- w_o: bfloat16 [4096, 4096], replicated
- q_gain: bfloat16 [128], replicated
- k_gain: bfloat16 [128], replicated
Outputs:
- output: bfloat16 [8192, 4096], P(('dp', 'sp')), parts along dimension 0
There are 4 independent parts. A program takes and returns all parts, laid end to end along the dimension named above; an argument that names none is the same for every part.
All inputs are finite; a program needn't handle non-finite values.
Results may differ from a plain program's by a relative error of at most 0.00695388.
Values are sent between devices in bfloat16 or wider.
A program may use at most 768 MiB of HBM per device.

v0:
```python
import jax
import jax.numpy as jnp
from jax import lax
from jax.sharding import PartitionSpec as P

EPS = 1e-6
THETA = 1000000.0


def head_norm(values, gain):
    return values * lax.rsqrt(jnp.mean(values * values, axis=-1, keepdims=True) + EPS) * gain.astype(jnp.float32)


def rotate(values, positions):
    head_dim = values.shape[-1]
    half = head_dim // 2
    inv_freq = jnp.power(THETA, -(jnp.arange(half, dtype=jnp.float32) * (2.0 / head_dim)))
    angles = positions.astype(jnp.float32)[:, None] * inv_freq[None, :]
    cos_pos = jnp.cos(angles)[:, None, :]
    sin_pos = jnp.sin(angles)[:, None, :]
    first_half = values[..., :half]
    second_half = values[..., half:]
    return jnp.concatenate([first_half * cos_pos - second_half * sin_pos, second_half * cos_pos + first_half * sin_pos], axis=-1)


def project(hidden, ln_gain, w_q, w_k, w_v, q_gain, k_gain, positions):
    tokens = hidden.shape[0]
    head_dim = q_gain.shape[0]
    hidden_f32 = hidden.astype(jnp.float32)
    normed = (hidden_f32 * lax.rsqrt(jnp.mean(hidden_f32 * hidden_f32, axis=-1, keepdims=True) + EPS) * ln_gain.astype(jnp.float32)).astype(jnp.bfloat16)
    q_raw = jnp.dot(normed, w_q, preferred_element_type=jnp.float32).reshape(tokens, -1, head_dim)
    k_raw = jnp.dot(normed, w_k, preferred_element_type=jnp.float32).reshape(tokens, -1, head_dim)
    v_local = jnp.dot(normed, w_v, preferred_element_type=jnp.float32).astype(jnp.bfloat16).reshape(tokens, -1, head_dim)
    q_local = rotate(head_norm(q_raw, q_gain), positions).astype(jnp.bfloat16)
    k_local = rotate(head_norm(k_raw, k_gain), positions).astype(jnp.bfloat16)
    return hidden_f32, q_local, k_local, v_local


def attend(q_all, k_all, v_all, q_start):
    q_rows, q_heads, head_dim = q_all.shape
    k_rows = k_all.shape[0]
    k_heads = k_all.shape[1]
    group = q_heads // k_heads
    limit = 2 ** 25 // (q_heads * k_rows)
    block_rows = min(q_rows, 2 ** max(3, min(9, limit.bit_length() - 1)))
    num_blocks = q_rows // block_rows
    q_blocks = q_all.reshape(num_blocks, block_rows, k_heads, group, head_dim)
    key_pos = jnp.arange(k_rows)
    score_scale = head_dim ** -0.5

    def one_block(block_args):
        q_block, block_idx = block_args
        scores = jnp.einsum('qkgd,skd->kgqs', q_block, k_all, preferred_element_type=jnp.float32) * score_scale
        q_pos = q_start + block_idx * block_rows + jnp.arange(block_rows)
        visible = q_pos[:, None] >= key_pos[None, :]
        scores = jnp.where(visible, scores, -jnp.inf)
        attn_prob = jax.nn.softmax(scores, axis=-1).astype(jnp.bfloat16)
        mixed = jnp.einsum('kgqs,skd->qkgd', attn_prob, v_all, preferred_element_type=jnp.float32)
        return mixed.astype(jnp.bfloat16)

    outputs = lax.map(one_block, (q_blocks, jnp.arange(num_blocks)))
    return outputs.reshape(q_rows, q_heads, head_dim)


def finish(hidden_f32, mixed, w_o):
    tokens = mixed.shape[0]
    result = hidden_f32 + jnp.dot(mixed.reshape(tokens, -1), w_o, preferred_element_type=jnp.float32)
    return result.astype(jnp.bfloat16)


def solution(mesh):
    group_size = mesh.shape['sp']

    def device_step(hidden, ln_gain, w_q, w_k, w_v, w_o, q_gain, k_gain):
        tokens = hidden.shape[0]
        head_dim = q_gain.shape[0]
        kv_heads = w_k.shape[1] // head_dim
        copies = max(1, group_size // kv_heads)
        positions = lax.axis_index('sp') * tokens + jnp.arange(tokens)
        hidden_f32, q_local, k_local, v_local = project(hidden, ln_gain, w_q, w_k, w_v, q_gain, k_gain, positions)
        q_heads = lax.all_to_all(q_local, 'sp', 1, 0, tiled=True)
        k_heads = lax.all_to_all(jnp.repeat(k_local, copies, axis=1), 'sp', 1, 0, tiled=True)
        v_heads = lax.all_to_all(jnp.repeat(v_local, copies, axis=1), 'sp', 1, 0, tiled=True)
        mixed = attend(q_heads, k_heads, v_heads, 0)
        mixed_local = lax.all_to_all(mixed, 'sp', 0, 1, tiled=True)
        return finish(hidden_f32, mixed_local, w_o)

    row_spec = P(('dp', 'sp'), None)
    return jax.shard_map(device_step, mesh=mesh, in_specs=(row_spec, P(), P(), P(), P(), P(), P(), P()), out_specs=row_spec, check_vma=False)
```

profile of v0, /device:TPU:21, one launch (start us, length us, event | category | flops | bytes accessed | tf_op | source)
XLA Modules:
  0.0 191.3 jit_solution(7839351255718461972)
XLA Ops:
  0.0 0.7 convert_element_type.47
  0.7 1.5 fusion.24
  2.3 5.0 %convolution_bitcast_fusion = f32[16,8,8,128]{3,1,2,0:T(8,128)S(1)} fusion(bf16[4096,1024]{1,0:T(8,128)(2,1)} %param.13, bf16[128,4096]{1,0:T(8,128)(2,1)} %param.10, f32[4096]{0:T(1024)S(1)} %convert_element_type.47, f32[128]{0:T(128)S(1)} %add_rsqrt_fusion.2), kind=kOutput, calls=%fused_computation.33 | convolution fusion | flops 1075838976 | bytes 9978368 | tf_op jit(solution)/shard_map/dot_general | solution.py:32
  8.8 0.9 broadcast_in_dim.16
  9.7 10.7 %all-to-all-start.1 = ((bf16[128,16,128]{2,0,1:T(8,128)(2,1)}), bf16[128,16,128]{2,0,1:T(8,128)(2,1)}, u32[]{:S(2)}, u32[]{:S(2)}) async-start(bf16[128,16,128]{2,0,1:T(8,128)(2,1)} %bitcast.3), calls=%async_computation.1 | async-start | bytes 1048576 | tf_op jit(solution)/shard_map/all_to_all | solution.py:82
  20.5 13.0 %fusion.31 = f32[128,4096]{1,0:T(8,128)S(1)} fusion(bf16[4096,4096]{1,0:T(8,128)(2,1)} %param.12, bf16[128,4096]{1,0:T(8,128)(2,1)S(1)} %copy-done, f32[4096]{0:T(1024)S(1)} %convert_element_type.47, f32[128]{0:T(128)S(1)} %add_rsqrt_fusion.2), kind=kOutput, calls=%fused_computation.50 | convolution fusion | flops 4297064448 | bytes 36717056 | tf_op jit(solution)/shard_map/dot_general | solution.py:31
  34.5 0.7 fusion.27
  35.2 0.8 subtract_convert_fusion
  36.0 1.6 pad_maximum_fusion
  37.6 7.2 %all-to-all-start = ((bf16[128,32,128]{2,0,1:T(8,128)(2,1)}), bf16[128,32,128]{2,0,1:T(8,128)(2,1)S(1)}, u32[]{:S(2)}, u32[]{:S(2)}) async-start(bf16[128,32,128]{2,0,1:T(8,128)(2,1)} %pad_maximum_fusion), calls=%async_computation | async-start | bytes 2097152 | tf_op jit(solution)/shard_map/all_to_all | solution.py:81
  44.8 4.7 %fusion.28 = bf16[16,8,8,128]{3,2,1,0:T(8,128)(2,1)S(1)} fusion(bf16[4096,1024]{1,0:T(8,128)(2,1)} %param.14, bf16[128,4096]{1,0:T(8,128)(2,1)S(1)} %copy-done, f32[4096]{0:T(1024)S(1)} %convert_element_type.47, f32[128]{0:T(128)S(1)} %add_rsqrt_fusion.2), kind=kOutput, calls=%fused_computation.35 | convolution fusion | flops 1075970048 | bytes 9716224 | tf_op jit(solution)/shard_map/dot_general | solution.py:33
  49.6 23.1 %all-to-all-done = bf16[128,32,128]{2,0,1:T(8,128)(2,1)S(1)} async-done(((bf16[128,32,128]{2,0,1:T(8,128)(2,1)}), bf16[128,32,128]{2,0,1:T(8,128)(2,1)S(1)}, u32[]{:S(2)}, u32[]{:S(2)}) %all-to-all-start) | async-done | bytes 1048608 | tf_op jit(solution)/shard_map/all_to_all | solution.py:81
  72.7 0.9 broadcast_in_dim.17
  73.6 4.5 %all-to-all-start.2 = ((bf16[128,16,128]{2,0,1:T(8,128)(2,1)}), bf16[128,16,128]{2,0,1:T(8,128)(2,1)}, u32[]{:S(2)}, u32[]{:S(2)}) async-start(bf16[128,16,128]{2,0,1:T(8,128)(2,1)} %bitcast.7), calls=%async_computation.2 | async-start | bytes 1048576 | tf_op jit(solution)/shard_map/all_to_all | solution.py:83
  78.3 16.7 %all-to-all-done.2 = bf16[128,16,128]{2,0,1:T(8,128)(2,1)} async-done(((bf16[128,16,128]{2,0,1:T(8,128)(2,1)}), bf16[128,16,128]{2,0,1:T(8,128)(2,1)}, u32[]{:S(2)}, u32[]{:S(2)}) %all-to-all-start.2) | async-done | bytes 524320 | tf_op jit(solution)/shard_map/all_to_all | solution.py:83
  95.0 48.3 %while.11 = (s32[]{:T(128)}, bf16[4,512,1,2,128]{4,1,0,3,2:T(8,128)(2,1)}, s32[4]{0:T(128)S(1)}, bf16[4,512,1,2,128]{4,1,0,3,2:T(8,128)(2,1)S(1)}, bf16[2048,1,1...) while((s32[]{:T(128)}, ...), condition=%wide.region_6.7_spmd.clone, body=%wide.region_3.6_spmd.clone.sunk | while | flops 1100085760 | bytes 30958196 | solution.py:61
  97.0 3.0 %fusion.46 = (f32[2,512]{1,0:T(2,128)S(1)}, f32[512,2,2048]{2,0,1:T(8,128)S(1)}) fusion(pred[512,2048]{1,0:T(8,128)(4,1)S(1)} %iota_compare_fusion.2, bf16[2048,1,128]{2,0,1:T(8,128)(2,1)} %get-tuple-element.174, bf16[4,512,1,2,128]{4,1,0,3,2:T(8,128)(2,1)S(1)} %get-tuple-element.173, s32[]{:T(128)} %get-tuple-element.162), kind=kOutput, calls=%fused_computation.5.clone.1 | convolution fusion | flops 543161344 | bytes 10227716 | tf_op jit(solution)/shard_map/while/body/eval_jaxpr/qkgd,skd->kgqs/dot_general | solution.py:53
  99.9 2.5 %fusion.47 = f32[2,512]{1,0:T(2,128)S(1)} fusion(f32[512,2,2048]{2,0,1:T(8,128)S(1)} %get-tuple-element.152, f32[2,512]{1,0:T(2,128)S(1)} %get-tuple-element.153, pred[512,2048]{1,0:T(8,128)(4,1)S(1)} %iota_compare_fusion.2), kind=kLoop, calls=%fused_computation.4.clone.1 | loop fusion | flops 8387584 | bytes 9445376 | tf_op jit(solution)/shard_map/while/body/eval_jaxpr/reduce_sum | solution.py:57
  102.5 4.6 %fusion.48 = bf16[4,512,1,2,128]{4,1,0,3,2:T(8,128)(2,1)} fusion(bf16[4,512,1,2,128]{4,1,0,3,2:T(8,128)(2,1)} %get-tuple-element.163, s32[]{:T(128)} %get-tuple-element.162, f32[2,512]{1,0:T(2,128)S(1)} %fusion.47, f32[2,512]{1,0:T(2,128)S(1)} %get-tuple-element.153, f32[512,2,2048]{2,0,1:T(8,128)S(1)} %get-tuple-element.152, ...), kind=kOutput, calls=%fused_computation.11.clone.1 | convolution fusion | flops 547487744 | bytes 10232320 | tf_op jit(solution)/shard_map/while/body/eval_jaxpr/kgqs,skd->qkgd/dot_general | solution.py:58
  109.1 3.0 %fusion.46 = (f32[2,512]{1,0:T(2,128)S(1)}, f32[512,2,2048]{2,0,1:T(8,128)S(1)}) fusion(pred[512,2048]{1,0:T(8,128)(4,1)S(1)} %iota_compare_fusion.2, bf16[2048,1,128]{2,0,1:T(8,128)(2,1)} %get-tuple-element.174, bf16[4,512,1,2,128]{4,1,0,3,2:T(8,128)(2,1)S(1)} %get-tuple-element.173, s32[]{:T(128)} %get-tuple-element.162), kind=kOutput, calls=%fused_computation.5.clone.1 | convolution fusion | flops 543161344 | bytes 10227716 | tf_op jit(solution)/shard_map/while/body/eval_jaxpr/qkgd,skd->kgqs/dot_general | solution.py:53
  112.0 2.5 %fusion.47 = f32[2,512]{1,0:T(2,128)S(1)} fusion(f32[512,2,2048]{2,0,1:T(8,128)S(1)} %get-tuple-element.152, f32[2,512]{1,0:T(2,128)S(1)} %get-tuple-element.153, pred[512,2048]{1,0:T(8,128)(4,1)S(1)} %iota_compare_fusion.2), kind=kLoop, calls=%fused_computation.4.clone.1 | loop fusion | flops 8387584 | bytes 9445376 | tf_op jit(solution)/shard_map/while/body/eval_jaxpr/reduce_sum | solution.py:57
  114.5 4.6 %fusion.48 = bf16[4,512,1,2,128]{4,1,0,3,2:T(8,128)(2,1)} fusion(bf16[4,512,1,2,128]{4,1,0,3,2:T(8,128)(2,1)} %get-tuple-element.163, s32[]{:T(128)} %get-tuple-element.162, f32[2,512]{1,0:T(2,128)S(1)} %fusion.47, f32[2,512]{1,0:T(2,128)S(1)} %get-tuple-element.153, f32[512,2,2048]{2,0,1:T(8,128)S(1)} %get-tuple-element.152, ...), kind=kOutput, calls=%fused_computation.11.clone.1 | convolution fusion | flops 547487744 | bytes 10232320 | tf_op jit(solution)/shard_map/while/body/eval_jaxpr/kgqs,skd->qkgd/dot_general | solution.py:58
  121.1 3.0 %fusion.46 = (f32[2,512]{1,0:T(2,128)S(1)}, f32[512,2,2048]{2,0,1:T(8,128)S(1)}) fusion(pred[512,2048]{1,0:T(8,128)(4,1)S(1)} %iota_compare_fusion.2, bf16[2048,1,128]{2,0,1:T(8,128)(2,1)} %get-tuple-element.174, bf16[4,512,1,2,128]{4,1,0,3,2:T(8,128)(2,1)S(1)} %get-tuple-element.173, s32[]{:T(128)} %get-tuple-element.162), kind=kOutput, calls=%fused_computation.5.clone.1 | convolution fusion | flops 543161344 | bytes 10227716 | tf_op jit(solution)/shard_map/while/body/eval_jaxpr/qkgd,skd->kgqs/dot_general | solution.py:53
  124.1 2.5 %fusion.47 = f32[2,512]{1,0:T(2,128)S(1)} fusion(f32[512,2,2048]{2,0,1:T(8,128)S(1)} %get-tuple-element.152, f32[2,512]{1,0:T(2,128)S(1)} %get-tuple-element.153, pred[512,2048]{1,0:T(8,128)(4,1)S(1)} %iota_compare_fusion.2), kind=kLoop, calls=%fused_computation.4.clone.1 | loop fusion | flops 8387584 | bytes 9445376 | tf_op jit(solution)/shard_map/while/body/eval_jaxpr/reduce_sum | solution.py:57
  126.6 4.6 %fusion.48 = bf16[4,512,1,2,128]{4,1,0,3,2:T(8,128)(2,1)} fusion(bf16[4,512,1,2,128]{4,1,0,3,2:T(8,128)(2,1)} %get-tuple-element.163, s32[]{:T(128)} %get-tuple-element.162, f32[2,512]{1,0:T(2,128)S(1)} %fusion.47, f32[2,512]{1,0:T(2,128)S(1)} %get-tuple-element.153, f32[512,2,2048]{2,0,1:T(8,128)S(1)} %get-tuple-element.152, ...), kind=kOutput, calls=%fused_computation.11.clone.1 | convolution fusion | flops 547487744 | bytes 10232320 | tf_op jit(solution)/shard_map/while/body/eval_jaxpr/kgqs,skd->qkgd/dot_general | solution.py:58
  133.2 3.0 %fusion.46 = (f32[2,512]{1,0:T(2,128)S(1)}, f32[512,2,2048]{2,0,1:T(8,128)S(1)}) fusion(pred[512,2048]{1,0:T(8,128)(4,1)S(1)} %iota_compare_fusion.2, bf16[2048,1,128]{2,0,1:T(8,128)(2,1)} %get-tuple-element.174, bf16[4,512,1,2,128]{4,1,0,3,2:T(8,128)(2,1)S(1)} %get-tuple-element.173, s32[]{:T(128)} %get-tuple-element.162), kind=kOutput, calls=%fused_computation.5.clone.1 | convolution fusion | flops 543161344 | bytes 10227716 | tf_op jit(solution)/shard_map/while/body/eval_jaxpr/qkgd,skd->kgqs/dot_general | solution.py:53
  136.2 2.5 %fusion.47 = f32[2,512]{1,0:T(2,128)S(1)} fusion(f32[512,2,2048]{2,0,1:T(8,128)S(1)} %get-tuple-element.152, f32[2,512]{1,0:T(2,128)S(1)} %get-tuple-element.153, pred[512,2048]{1,0:T(8,128)(4,1)S(1)} %iota_compare_fusion.2), kind=kLoop, calls=%fused_computation.4.clone.1 | loop fusion | flops 8387584 | bytes 9445376 | tf_op jit(solution)/shard_map/while/body/eval_jaxpr/reduce_sum | solution.py:57
  138.7 4.6 %fusion.48 = bf16[4,512,1,2,128]{4,1,0,3,2:T(8,128)(2,1)} fusion(bf16[4,512,1,2,128]{4,1,0,3,2:T(8,128)(2,1)} %get-tuple-element.163, s32[]{:T(128)} %get-tuple-element.162, f32[2,512]{1,0:T(2,128)S(1)} %fusion.47, f32[2,512]{1,0:T(2,128)S(1)} %get-tuple-element.153, f32[512,2,2048]{2,0,1:T(8,128)S(1)} %get-tuple-element.152, ...), kind=kOutput, calls=%fused_computation.11.clone.1 | convolution fusion | flops 547487744 | bytes 10232320 | tf_op jit(solution)/shard_map/while/body/eval_jaxpr/kgqs,skd->qkgd/dot_general | solution.py:58
  143.3 2.8 %copy.61 = bf16[2048,2,128]{2,1,0:T(2,128)(2,1)S(1)} copy(bf16[2048,2,128]{2,0,1:T(8,128)(2,1)} %bitcast.130) | data formatting | bytes 2097152 | tf_op jit(solution)/shard_map/reshape | solution.py:62
  146.1 30.3 %all_to_all.66 = bf16[2048,2,128]{2,1,0:T(2,128)(2,1)S(1)} all-to-all(bf16[2048,2,128]{2,1,0:T(2,128)(2,1)S(1)} %copy.61), channel_id=1, replica_groups=mesh['dp'=4,'sp'=16] {'sp'}, dimensions={0} | all-to-all | bytes 2097152 | tf_op jit(solution)/shard_map/all_to_all | solution.py:85
  176.5 0.7 copy.63
  177.2 14.1 %fusion.23 = bf16[128,4096]{1,0:T(8,128)(2,1)} fusion(bf16[128,4096]{0,1:T(8,128)(2,1)S(1)} %bitcast.124, bf16[4096,4096]{1,0:T(8,128)(2,1)} %param.15, bf16[128,4096]{1,0:T(8,128)(2,1)S(1)} %copy-done), kind=kOutput, calls=%fused_computation.22 | convolution fusion | flops 4296540160 | bytes 36700160 | tf_op jit(solution)/shard_map/dot_general | solution.py:67
  (43 shorter events, 8.1 us)
Async XLA Ops:
  2.3 5.5 %copy-start.1 = (bf16[128]{0:T(256)(128)(2,1)S(1)}, bf16[128]{0:T(256)(128)(2,1)}, u32[]{:S(2)}) copy-start(bf16[128]{0:T(256)(128)(2,1)} %param.17) | copy-start | bytes 772
  8.3 12.1 %copy-start = (bf16[128,4096]{1,0:T(8,128)(2,1)S(1)}, bf16[128,4096]{1,0:T(8,128)(2,1)}, u32[]{:S(2)}) copy-start(bf16[128,4096]{1,0:T(8,128)(2,1)} %param.10) | copy-start | bytes 3145732
  9.7 27.9 %all-to-all-start.1 = ((bf16[128,16,128]{2,0,1:T(8,128)(2,1)}), bf16[128,16,128]{2,0,1:T(8,128)(2,1)}, u32[]{:S(2)}, u32[]{:S(2)}) async-start(bf16[128,16,128]{2,0,1:T(8,128)(2,1)} %bitcast.3), calls=%async_computation.1 | async-start | bytes 1048576 | tf_op jit(solution)/shard_map/all_to_all | solution.py:82
  33.8 0.7 copy-start.2
  37.6 35.1 %all-to-all-start = ((bf16[128,32,128]{2,0,1:T(8,128)(2,1)}), bf16[128,32,128]{2,0,1:T(8,128)(2,1)S(1)}, u32[]{:S(2)}, u32[]{:S(2)}) async-start(bf16[128,32,128]{2,0,1:T(8,128)(2,1)} %pad_maximum_fusion), calls=%async_computation | async-start | bytes 2097152 | tf_op jit(solution)/shard_map/all_to_all | solution.py:81
  73.6 21.3 %all-to-all-start.2 = ((bf16[128,16,128]{2,0,1:T(8,128)(2,1)}), bf16[128,16,128]{2,0,1:T(8,128)(2,1)}, u32[]{:S(2)}, u32[]{:S(2)}) async-start(bf16[128,16,128]{2,0,1:T(8,128)(2,1)} %bitcast.7), calls=%async_computation.2 | async-start | bytes 1048576 | tf_op jit(solution)/shard_map/all_to_all | solution.py:83
where the time goes:
time: 192 us; the launch traced here: 191 us
  matrix products  66.9 us (35%)
  waiting for transfers between devices  39.8 us (21%)
  blocking collectives  30.3 us (16%)
  starting transfers between devices  22.5 us (12%)
  other arithmetic  19.8 us (10%)
  local copies, waits for them, and re-layouts  9 us (5%)
  loops' own time  2.86 us (1%)
    all_to_all x1, blocking collectives, device_step(): mixed_local = lax.all_to_all(mixed, 'sp', 0, 1, tiled=True)  30.3 us
    all_to_all x1, waiting for transfers between devices, device_step(): q_heads = lax.all_to_all(q_local, 'sp', 1, 0, tiled=True)  23.1 us
    dot_general x4, matrix products, one_block(): jnp.einsum('kgqs,skd->qkgd', attn_prob, v_all, preferred_element_type=jnp...  18.3 us
    all_to_all x1, waiting for transfers between devices, device_step(): lax.all_to_all(jnp.repeat(v_local, copies, axis=1), 'sp', 1, 0, tiled=True)  16.7 us
    dot_general x1, matrix products, finish(): jnp.dot(mixed.reshape(tokens, -1), w_o, preferred_element_type=jnp.float32)  14.1 us
    dot_general x1, matrix products, project(): jnp.dot(normed, w_q, preferred_element_type=jnp.float32)  13 us
    dot_general x4, matrix products, one_block(): jnp.einsum('qkgd,skd->kgqs', q_block, k_all, preferred_element_type=jnp.f...  11.8 us
    all_to_all x1, starting transfers between devices, device_step(): lax.all_to_all(jnp.repeat(k_local, copies, axis=1), 'sp', 1, 0, tiled=True)  10.7 us
  transfers between devices with their start and end apart: 3, of which 2 were waited for; matrix products, arithmetic and copies ran while one was open for 11% of the time, Pallas kernels for 0%

commit v1 on v0

v1 whole, which is shorter than its diff:
```python
import functools
import jax
import jax.numpy as jnp
from jax import lax
from jax.experimental import pallas as pl
from jax.experimental.pallas import tpu as pltpu
from jax.sharding import PartitionSpec as P

EPS = 1e-6
THETA = 1000000.0
LOG2E = 1.4426950408889634
CORES = 2
BF16 = jnp.bfloat16
F32 = jnp.float32


def dot(a, b):
    return jnp.dot(a, b, preferred_element_type=F32)


def kernel(group_size, x_hbm, wq, wk, wv, wo, ln_gain, q_gain_t, k_gain, cos_k, sin_k, cos_t, sin_t, out_ref,
           x_buf, h_buf, w_buf, wo_buf, kv, stage, q_t, o_t, m_buf, l_buf, o_all, o_send,
           x_sem, w_sem, wo_sem, h_ssem, h_rsem, d2d_ssem, d2d_rsem, first_ssem, first_rsem, ring_ssem, ring_rsem, o_ssem, o_rsem):
    chips = group_size // CORES
    me = lax.axis_index('sp')
    chip = me // CORES
    core = me % CORES
    partner = chip * CORES + (1 - core)
    rows = x_buf.shape[0]
    dim = x_buf.shape[1]
    head = k_gain.shape[1]
    half_head = head // 2
    width = w_buf.shape[2]
    local_heads = kv.shape[1]
    group = width // head
    chip_rows = rows * CORES
    far = chips // 2

    def device(c, k):
        return {'sp': c * CORES + k}

    def neighbour(dirn):
        return (chip + chips + 1 - 2 * dirn) % chips

    barrier = pltpu.get_barrier_semaphore()
    pl.semaphore_signal(barrier, inc=1, device_id={'sp': partner})
    for dirn in range(2):
        for k in range(CORES):
            pl.semaphore_signal(barrier, inc=1, device_id=device(neighbour(dirn), k))

    x_copy = pltpu.make_async_copy(x_hbm, x_buf, x_sem)
    x_copy.start()

    def kv_copies(idx):
        pair = (idx % 2) * 2 + idx // 2
        cols = pl.ds(pl.multiple_of(pair * (width // 2), width // 2), width // 2)
        slot = idx % 3
        return (pltpu.make_async_copy(wk.at[:, cols], w_buf.at[slot, :, pl.ds(0, width // 2)], w_sem.at[slot, 0]),
                pltpu.make_async_copy(wv.at[:, cols], w_buf.at[slot, :, pl.ds(width // 2, width // 2)], w_sem.at[slot, 1]))

    def q_copies(idx):
        cols = pl.ds(pl.multiple_of((core * local_heads + idx) * width, width), width)
        slot = (idx + 4) % 3
        return tuple(pltpu.make_async_copy(wq.at[pl.ds(r * (dim // 2), dim // 2), cols],
                                           w_buf.at[slot, pl.ds(r * (dim // 2), dim // 2), :], w_sem.at[slot, r]) for r in range(2))

    def wo_copy(b):
        return pltpu.make_async_copy(wo.at[pl.ds(b * width, width), :], wo_buf.at[pl.ds(b * width, width), :], wo_sem.at[b])

    for idx in range(3):
        for copy in kv_copies(idx):
            copy.start()

    x_copy.wait()
    step_rows = 16

    def norm_rows(r, carry):
        sl = pl.ds(pl.multiple_of(r * step_rows, step_rows), step_rows)
        xf = x_buf[sl, :].astype(F32)
        scale = lax.rsqrt(jnp.mean(xf * xf, axis=-1, keepdims=True) + EPS)
        h_buf[core, sl, :] = (xf * scale * ln_gain[...]).astype(BF16)
        return carry

    lax.fori_loop(0, rows // step_rows, norm_rows, 0)

    pl.semaphore_wait(barrier, 1 + 2 * CORES)
    h_copy = pltpu.make_async_remote_copy(h_buf.at[core], h_buf.at[core], h_ssem, h_rsem, device_id={'sp': partner})
    h_copy.start()

    def down_reach(j):
        return far - 1 + j // 2

    def first_copies(idx, e):
        owner = idx % 2
        j = (idx // 2) * 2 + e
        src = stage.at[idx, e]
        dst = kv.at[chip, j, core]
        up = pltpu.make_async_remote_copy(src, dst, first_ssem.at[0, idx, e], first_rsem.at[0, j, core], device_id=device(neighbour(0), owner))
        down = pltpu.make_async_remote_copy(src, dst, first_ssem.at[1, idx, e], first_rsem.at[1, j, core], device_id=device(neighbour(1), owner))
        across = pltpu.make_async_remote_copy(src, dst, d2d_ssem.at[j], d2d_rsem.at[j], device_id={'sp': partner})
        return ((up, chip < chips - 1), (down, chip < down_reach(j)), (across, owner != core))

    def project_kv(idx, carry):
        slot = idx % 3
        for copy in kv_copies(idx):
            copy.wait()
        raw = dot(h_buf[core], w_buf[slot])

        @pl.when(idx == 0)
        def _():
            for copy in kv_copies(3):
                copy.start()

        @pl.when(idx > 0)
        def _():
            for copy in q_copies(idx - 1):
                copy.start()

        for e in range(2):
            t = raw[:, e * head:(e + 1) * head]
            t = t * lax.rsqrt(jnp.mean(t * t, axis=-1, keepdims=True) + EPS) * k_gain[...]
            k_val = (t * cos_k[...] + pltpu.roll(t, half_head, 1) * sin_k[...]).astype(BF16)
            v_val = raw[:, width // 2 + e * head:width // 2 + (e + 1) * head].T.astype(BF16)
            stage[idx, e, 0] = k_val
            stage[idx, e, 1] = v_val

            @pl.when(idx % 2 == core)
            def _():
                kv[chip, (idx // 2) * 2 + e, core, 0] = k_val
                kv[chip, (idx // 2) * 2 + e, core, 1] = v_val

        for e in range(2):
            for copy, cond in first_copies(idx, e):
                pl.when(cond)(copy.start)
        return carry

    lax.fori_loop(0, 4, project_kv, 0)
    for b in range(wo_sem.shape[0]):
        wo_copy(b).start()
    h_copy.wait_recv()

    def project_q(idx, carry):
        slot = (idx + 4) % 3
        for copy in q_copies(idx):
            copy.wait()
        raw = dot(h_buf[...].reshape(chip_rows, dim), w_buf[slot])

        @pl.when(idx == 0)
        def _():
            for copy in q_copies(3):
                copy.start()

        for g in range(group):
            t = raw[:, g * head:(g + 1) * head].T
            t = t * lax.rsqrt(jnp.mean(t * t, axis=0, keepdims=True) + EPS) * q_gain_t[...]
            t1 = t[:half_head]
            t2 = t[half_head:]
            c = cos_t[...]
            s = sin_t[...]
            q_t[idx, :, g * chip_rows:(g + 1) * chip_rows] = jnp.concatenate([t1 * c - t2 * s, t2 * c + t1 * s], axis=0).astype(BF16)
        return carry

    lax.fori_loop(0, local_heads, project_q, 0)

    score_scale = (head ** -0.5) * LOG2E

    def attend(item, j, first):
        keys = kv[item, j, :, 0].reshape(chip_rows, head)
        vals = jnp.concatenate([kv[item, j, 0, 1], kv[item, j, 1, 1]], axis=1)
        for g in range(group):
            cols = slice(g * chip_rows, (g + 1) * chip_rows)
            scores = dot(keys, q_t[j, :, cols])
            if first:
                key_pos = lax.broadcasted_iota(jnp.int32, scores.shape, 0)
                q_pos = lax.broadcasted_iota(jnp.int32, scores.shape, 1)
                scores = jnp.where(key_pos <= q_pos, scores, -jnp.inf)
                m_new = jnp.max(scores, axis=0, keepdims=True)
            else:
                m_old = m_buf[j, :, cols]
                m_new = jnp.maximum(m_old, jnp.max(scores, axis=0, keepdims=True))
            prob = jnp.exp2((scores - m_new) * score_scale)
            total = jnp.sum(prob, axis=0, keepdims=True)
            mixed = dot(vals, prob.astype(BF16))
            m_buf[j, :, cols] = m_new
            if first:
                l_buf[j, :, cols] = total
                o_t[j, :, cols] = mixed
            else:
                alpha = jnp.exp2((m_old - m_new) * score_scale)
                l_buf[j, :, cols] = l_buf[j, :, cols] * alpha + total
                o_t[j, :, cols] = o_t[j, :, cols] * alpha + mixed

    def diagonal(j, carry):
        pltpu.make_async_remote_copy(kv.at[chip, j, 0], kv.at[chip, j, 1 - core], d2d_ssem.at[j], d2d_rsem.at[j], device_id={'sp': partner}).wait_recv()
        attend(chip, j, True)
        return carry

    lax.fori_loop(0, local_heads, diagonal, 0)

    def event(ev):
        dirn = ev % 2
        j = (ev // 2) % local_heads
        d = (ev // 2) // local_heads + 1
        reach = far - (dirn + j // 2) % 2
        item = (chip + chips + (2 * dirn - 1) * d) % chips
        valid = (d <= reach) & (((dirn == 0) & (item < chip)) | ((dirn == 1) & (item < reach)))
        forward = valid & (d + 1 <= reach) & ((dirn == 1) | (chip < chips - 1))
        return dirn, j, d, item, valid, forward

    def ring_copy(dirn, j, d, item):
        return pltpu.make_async_remote_copy(kv.at[item, j], kv.at[item, j], ring_ssem.at[dirn, d - 1, j], ring_rsem.at[dirn, d - 1, j],
                                            device_id=device(neighbour(dirn), core))

    def ring_step(ev, carry):
        dirn, j, d, item, valid, forward = event(ev)

        @pl.when(valid & (d == 1))
        def _():
            for k in range(CORES):
                pltpu.make_async_remote_copy(stage.at[0, 0], kv.at[item, j, k], first_ssem.at[0, 0, 0], first_rsem.at[dirn, j, k],
                                             device_id={'sp': partner}).wait_recv()

        @pl.when(valid & (d > 1))
        def _():
            ring_copy(dirn, j, d - 1, item).wait_recv()

        @pl.when(forward)
        def _():
            ring_copy(dirn, j, d, item).start()

        @pl.when(valid & (item < chip))
        def _():
            attend(item, j, False)

        return carry

    events = 2 * local_heads * far
    lax.fori_loop(0, events, ring_step, 0)

    def o_copy(j):
        cols = pl.ds(pl.multiple_of(j * width, width), width)
        return pltpu.make_async_remote_copy(o_send.at[:, cols], o_all.at[core, :, cols], o_ssem.at[j], o_rsem.at[j], device_id={'sp': partner})

    for j in range(local_heads):
        inv = 1.0 / l_buf[j]
        for g in range(group):
            cols = slice(g * chip_rows, (g + 1) * chip_rows)
            o_val = (o_t[j, :, cols] * inv[:, cols]).T.astype(BF16)
            mine = jnp.where(core == 0, o_val[:rows], o_val[rows:])
            other = jnp.where(core == 0, o_val[rows:], o_val[:rows])
            out_cols = slice(j * width + g * head, j * width + (g + 1) * head)
            o_all[core, :, out_cols] = mine
            o_send[:, out_cols] = other
        o_copy(j).start()

    for b in range(wo_sem.shape[0]):
        wo_copy(b).wait()
    for j in range(local_heads):
        o_copy(j).wait_recv()

    mixed_dim = local_heads * width

    def finish(n, carry):
        cols = pl.ds(pl.multiple_of(n * width, width), width)
        total = dot(o_all[0], wo_buf[:mixed_dim, cols]) + dot(o_all[1], wo_buf[mixed_dim:, cols])
        out_ref[:, cols] = (x_buf[:, cols].astype(F32) + total).astype(BF16)
        return carry

    lax.fori_loop(0, dim // width, finish, 0)

    h_copy.wait_send()
    for j in range(local_heads):
        o_copy(j).wait_send()

    def drain_first(idx, carry):
        for e in range(2):
            for copy, cond in first_copies(idx, e):
                pl.when(cond)(copy.wait_send)
        return carry

    lax.fori_loop(0, 4, drain_first, 0)

    def drain_ring(ev, carry):
        dirn, j, d, item, valid, forward = event(ev)

        @pl.when(forward)
        def _():
            ring_copy(dirn, j, d, item).wait_send()

        return carry

    lax.fori_loop(0, events, drain_ring, 0)


def solution(mesh):
    group_size = mesh.shape['sp']

    def device_step(hidden, ln_gain, w_q, w_k, w_v, w_o, q_gain, k_gain):
        rows, dim = hidden.shape
        head = q_gain.shape[0]
        half = head // 2
        chips = group_size // CORES
        local_heads = w_k.shape[1] // head // CORES
        width = w_q.shape[1] // CORES // local_heads
        chip_rows = rows * CORES
        me = lax.axis_index('sp')
        inv_freq = jnp.power(THETA, -(jnp.arange(half, dtype=F32) * (2.0 / head)))
        angles = ((me // CORES) * chip_rows + jnp.arange(chip_rows)).astype(F32)[None, :] * inv_freq[:, None]
        cos_t = jnp.cos(angles)
        sin_t = jnp.sin(angles)
        own = (me * rows + jnp.arange(rows)).astype(F32)[:, None] * inv_freq[None, :]
        cos_own = jnp.cos(own)
        sin_own = jnp.sin(own)
        cos_k = jnp.concatenate([cos_own, cos_own], axis=1)
        sin_k = jnp.concatenate([-sin_own, sin_own], axis=1)
        q_gain_t = jnp.broadcast_to(q_gain.astype(F32)[:, None], (head, chip_rows))
        vmem = pl.BlockSpec(memory_space=pltpu.VMEM)
        hbm = pl.BlockSpec(memory_space=pl.ANY)
        dma = pltpu.SemaphoreType.DMA
        return pl.pallas_call(
            functools.partial(kernel, group_size),
            out_shape=jax.ShapeDtypeStruct((rows, dim), BF16),
            in_specs=[hbm] * 5 + [vmem] * 7,
            out_specs=vmem,
            scratch_shapes=[
                pltpu.VMEM((rows, dim), BF16),
                pltpu.VMEM((CORES, rows, dim), BF16),
                pltpu.VMEM((3, dim, width), BF16),
                pltpu.VMEM(w_o.shape, BF16),
                pltpu.VMEM((chips, local_heads, CORES, 2, rows, head), BF16),
                pltpu.VMEM((4, 2, 2, rows, head), BF16),
                pltpu.VMEM((local_heads, head, width // head * chip_rows), BF16),
                pltpu.VMEM((local_heads, head, width // head * chip_rows), F32),
                pltpu.VMEM((local_heads, 1, width // head * chip_rows), F32),
                pltpu.VMEM((local_heads, 1, width // head * chip_rows), F32),
                pltpu.VMEM((CORES, rows, local_heads * width), BF16),
                pltpu.VMEM((rows, local_heads * width), BF16),
                dma, dma((3, 2)), dma((w_o.shape[0] // width,)), dma, dma,
                dma((local_heads,)), dma((local_heads,)),
                dma((2, 4, 2)), dma((2, local_heads, CORES)),
                dma((2, chips // 2, local_heads)), dma((2, chips // 2, local_heads)),
                dma((local_heads,)), dma((local_heads,)),
            ],
            compiler_params=pltpu.CompilerParams(collective_id=0, has_side_effects=True, vmem_limit_bytes=67043328),
        )(hidden, w_q, w_k, w_v, w_o, ln_gain.astype(F32)[None, :], q_gain_t, k_gain.astype(F32)[None, :], cos_k, sin_k, cos_t, sin_t)

    row_spec = P(('dp', 'sp'), None)
    return jax.shard_map(device_step, mesh=mesh, in_specs=(row_spec, P(), P(), P(), P(), P(), P(), P()), out_specs=row_spec, check_vma=False)
```

time: 192 us -> 86.5 us (0.45)
  the two profiles are of different devices: /device:TPU:21 before, /device:TPU:253 now
where the time goes in v1:
time: 86.5 us; the launch traced here: 86.4 us
  Pallas kernels  78.1 us (90%)
  other arithmetic  4.55 us (5%)
  local copies, waits for them, and re-layouts  3.68 us (4%)
    pallas_call x1, Pallas kernels, device_step(): pl.pallas_call(functools.partial(kernel, group_size), out_shape=jax.Shape...  78.1 us
    unnamed x1, local copies, waits for them, and re-layouts  2.29 us

profile of v1, /device:TPU:253, one launch (start us, length us, event | category | flops | bytes accessed | tf_op | source)
XLA Modules:
  0.0 86.4 jit_solution(15626526962583674399)
XLA Ops:
  0.0 1.2 %bitcast_convert_fusion.k_gain = f32[1,128]{1,0:T(1,128)} fusion(bf16[128]{0:T(256)(128)(2,1)} %param.15), kind=kLoop, calls=%fused_computation.8 | loop fusion | flops 128 | bytes 768 | tf_op jit(solution)/shard_map/broadcast_in_dim | solution.py:345
  1.2 1.3 %broadcast_in_dim.25 = f32[4096]{0:T(1024)} convert(bf16[4096]{0:T(1024)(128)(2,1)} %param.9) | non-fusion elementwise | flops 4096 | bytes 24576 | tf_op jit(solution)/shard_map/broadcast_in_dim | solution.py:345
  2.5 1.0 %multiply_sine_fusion = (f32[64,256]{1,0:T(8,128)}, f32[64,256]{1,0:T(8,128)}) fusion(f32[64]{0:T(128)S(1)} %negate_power_fusion, f32[256]{0:T(256)S(1)} %add_convert_fusion), kind=kLoop, calls=%fused_computation | loop fusion | flops 16384 | bytes 132352 | tf_op jit(solution)/shard_map/sin | solution.py:310
  3.5 1.4 %broadcast_in_dim.22.q_gain_t = f32[128,256]{1,0:T(8,128)} broadcast(bf16[128]{0:T(256)(128)(2,1)} %param.14), dimensions={0} | broadcast | bytes 131328 | tf_op jit(solution)/shard_map/broadcast_in_dim | solution.py:316
  4.9 0.3 fusion
  5.2 0.8 pad_maximum_fusion
  6.0 78.1 %shard_map.82 = bf16[128,4096]{1,0:T(8,128)(2,1)} custom-call(bf16[128,4096]{1,0:T(8,128)(2,1)} %x_hbm.1, bf16[4096,4096]{1,0:T(8,128)(2,1)} %wq.1, bf16[4096,1024]{1,0:T(8,128)(2,1)} %wk.1, bf16[4096,1024]{1,0:T(8,128)(2,1)} %wv.1, bf16[4096,4096]{1,0:T(8,128)(2,1)} %wo.1, f32[1,4096]{1,0:T(1,128)} %bitcast.4, f32[128,256]{1,0:T(8,128)} %broadcast_in_dim.22.q_gain_t, ...), custom_call_target="tpu_custom_call" | custom-call | tf_op jit(solution)/shard_map/pallas_call | solution.py:320
  84.1 2.3 %copy.10 = bf16[128,4096]{1,0:T(8,128)(2,1)} copy(bf16[128,4096]{1,0:T(8,128)(2,1)} %shard_map.82) | data formatting | bytes 2097152
  (3 shorter events, 0.0 us)

commit v2 on v1

v2 whole, which is shorter than its diff:
```python
import functools
import jax
import jax.numpy as jnp
import numpy as np
from jax import lax
from jax.experimental import pallas as pl
from jax.experimental.pallas import tpu as pltpu
from jax.sharding import PartitionSpec as P

EPS = 1e-6
THETA = 1000000.0
LOG2E = 1.4426950408889634
CORES = 2
BF16 = jnp.bfloat16
F32 = jnp.float32


def dot(a, b):
    return jnp.dot(a, b, preferred_element_type=F32)


def slot_table(values):
    return sum(v << (2 * s) for s, v in enumerate(values))


UP_HEAD = (0, 1, 2, 3, 0, 1, 2, 0, 1, 3, 0, 1, 2, 3)
UP_HOP = (0, 0, 0, 0, 1, 1, 1, 2, 2, 1, 3, 3, 2, 2)
DOWN_HEAD = (0, 1, 2, 3, 2, 3, 0, 1, 2, 3, 0, 1, 2, 3)
DOWN_HOP = (0, 0, 0, 0, 1, 1, 1, 1, 2, 2, 2, 2, 3, 3)
SLOTS = len(UP_HEAD)
TABLES = tuple(slot_table(t) for t in (UP_HEAD, UP_HOP, DOWN_HEAD, DOWN_HOP))
DRAIN_LAG = 7


def kernel(group_size, x_hbm, wq, wk, wv, wo, ln_hbm, q_gain_hbm, k_gain_hbm, cos_hbm, sin_hbm, out_hbm,
           x_buf, h_buf, w_buf, wo_buf, kv, stage, q_t, o_t, m_buf, l_buf, o_all, o_send, acc,
           ln_buf, gain_buf, cos_t, sin_t, gain_t, cos_k, sin_k,
           x_sem, small_sem, w_sem, wo_sem, h_ssem, h_rsem, d2d_ssem, d2d_rsem, first_ssem, first_rsem, ring_ssem, ring_rsem, o_ssem, o_rsem, out_sem):
    chips = group_size // CORES
    me = lax.axis_index('sp')
    chip = me // CORES
    core = me % CORES
    partner = chip * CORES + (1 - core)
    rows, dim = x_buf.shape
    head = gain_buf.shape[2]
    half_head = head // 2
    width = w_buf.shape[2]
    local_heads = kv.shape[1]
    group = width // head
    chip_rows = rows * CORES
    far = chips // 2
    mixed_dim = local_heads * width

    def device(c, k):
        return {'sp': c * CORES + k}

    def neighbour(dirn):
        return (chip + chips + 1 - 2 * dirn) % chips

    x_parts = x_sem.shape[0]
    part_rows = rows // x_parts

    def x_copy(r):
        sl = pl.ds(r * part_rows, part_rows)
        return pltpu.make_async_copy(x_hbm.at[sl, :], x_buf.at[sl, :], x_sem.at[r])

    chip_cols = pl.ds(pl.multiple_of(chip * chip_rows, chip_rows), chip_rows)
    small = (pltpu.make_async_copy(ln_hbm, ln_buf, small_sem.at[0]),
             pltpu.make_async_copy(q_gain_hbm, gain_buf.at[0], small_sem.at[1]),
             pltpu.make_async_copy(k_gain_hbm, gain_buf.at[1], small_sem.at[2]),
             pltpu.make_async_copy(cos_hbm.at[:, chip_cols], cos_t, small_sem.at[3]),
             pltpu.make_async_copy(sin_hbm.at[:, chip_cols], sin_t, small_sem.at[4]))

    def kv_copies(idx):
        pair = (idx % 2) * 2 + idx // 2
        cols = pl.ds(pl.multiple_of(pair * (width // 2), width // 2), width // 2)
        slot = idx % 3
        return (pltpu.make_async_copy(wk.at[:, cols], w_buf.at[slot, :, pl.ds(0, width // 2)], w_sem.at[slot, 0]),
                pltpu.make_async_copy(wv.at[:, cols], w_buf.at[slot, :, pl.ds(width // 2, width // 2)], w_sem.at[slot, 1]))

    def q_copies(idx):
        cols = pl.ds(pl.multiple_of((core * local_heads + idx) * width, width), width)
        slot = (idx + 4) % 3
        return tuple(pltpu.make_async_copy(wq.at[pl.ds(r * (dim // 2), dim // 2), cols],
                                           w_buf.at[slot, pl.ds(r * (dim // 2), dim // 2), :], w_sem.at[slot, r]) for r in range(2))

    def wo_copy(b):
        return pltpu.make_async_copy(wo.at[pl.ds(b * width, width), :], wo_buf.at[pl.ds(b * width, width), :], wo_sem.at[b])

    for copy in small[:1]:
        copy.start()
    for r in range(x_parts):
        x_copy(r).start()
    for copy in small[1:]:
        copy.start()
    for copy in kv_copies(0):
        copy.start()

    barrier = pltpu.get_barrier_semaphore()
    pl.semaphore_signal(barrier, inc=1, device_id={'sp': partner})
    for dirn in range(2):
        for k in range(CORES):
            pl.semaphore_signal(barrier, inc=1, device_id=device(neighbour(dirn), k))

    small[0].wait()
    for r in range(x_parts):
        x_copy(r).wait()
        if r == x_parts - 1:
            for idx in range(1, 3):
                for copy in kv_copies(idx):
                    copy.start()
        step_rows = 16
        for t in range(part_rows // step_rows):
            sl = slice(r * part_rows + t * step_rows, r * part_rows + (t + 1) * step_rows)
            xf = x_buf[sl, :].astype(F32)
            scale = lax.rsqrt(jnp.mean(xf * xf, axis=-1, keepdims=True) + EPS)
            h_buf[core, sl, :] = (xf * scale * ln_buf[...].astype(F32)).astype(BF16)

    for copy in small[1:]:
        copy.wait()
    gain_t[...] = jnp.broadcast_to(gain_buf[0].astype(F32), (chip_rows, head)).T
    own_cols = pl.ds(pl.multiple_of(core * rows, rows), rows)
    cos_own = cos_t[:, own_cols].T
    sin_own = sin_t[:, own_cols].T
    cos_k[...] = jnp.concatenate([cos_own, cos_own], axis=1)
    sin_k[...] = jnp.concatenate([-sin_own, sin_own], axis=1)

    pl.semaphore_wait(barrier, 1 + 2 * CORES)
    h_copy = pltpu.make_async_remote_copy(h_buf.at[core], h_buf.at[core], h_ssem, h_rsem, device_id={'sp': partner})

    def down_reach(j):
        return far - 1 + j // 2

    def first_copies(idx, e):
        owner = idx % 2
        j = (idx // 2) * 2 + e
        src = stage.at[idx, e]
        dst = kv.at[chip, j, core]
        up = pltpu.make_async_remote_copy(src, dst, first_ssem.at[0, idx, e], first_rsem.at[0, j, core], device_id=device(neighbour(0), owner))
        down = pltpu.make_async_remote_copy(src, dst, first_ssem.at[1, idx, e], first_rsem.at[1, j, core], device_id=device(neighbour(1), owner))
        across = pltpu.make_async_remote_copy(src, dst, d2d_ssem.at[j], d2d_rsem.at[j], device_id={'sp': partner})
        return ((up, chip < chips - 1), (down, chip < down_reach(j)), (across, owner != core))

    def project_kv(idx, carry):
        slot = idx % 3
        for copy in kv_copies(idx):
            copy.wait()
        raw = dot(h_buf[core], w_buf[slot])

        @pl.when(idx == 0)
        def _():
            for copy in kv_copies(3):
                copy.start()

        @pl.when(idx > 0)
        def _():
            for copy in q_copies(idx - 1):
                copy.start()

        for e in range(2):
            t = raw[:, e * head:(e + 1) * head]
            t = t * lax.rsqrt(jnp.mean(t * t, axis=-1, keepdims=True) + EPS) * gain_buf[1].astype(F32)
            k_val = (t * cos_k[...] + pltpu.roll(t, half_head, 1) * sin_k[...]).astype(BF16)
            v_val = raw[:, width // 2 + e * head:width // 2 + (e + 1) * head].T.astype(BF16)
            stage[idx, e, 0] = k_val
            stage[idx, e, 1] = v_val

            @pl.when(idx % 2 == core)
            def _():
                kv[chip, (idx // 2) * 2 + e, core, 0] = k_val
                kv[chip, (idx // 2) * 2 + e, core, 1] = v_val

        for e in range(2):
            for copy, cond in first_copies(idx, e):
                pl.when(cond)(copy.start)

        @pl.when(idx == 0)
        def _():
            h_copy.start()

        return carry

    lax.fori_loop(0, 4, project_kv, 0)
    h_copy.wait_recv()

    def event(s, dirn):
        j = lax.shift_right_logical(jnp.int32(TABLES[2 * dirn]), 2 * s) % 4
        d = lax.shift_right_logical(jnp.int32(TABLES[2 * dirn + 1]), 2 * s) % 4 + 1
        if dirn == 0:
            reach = far - j // 2
            item = (chip + chips - d) % chips
            valid = (d <= reach) & (item < chip)
            forward = valid & (d + 1 <= reach) & (chip < chips - 1)
        else:
            reach = far - 1 + j // 2
            item = (chip + d) % chips
            valid = (d <= reach) & (item < reach)
            forward = valid & (d + 1 <= reach)
        return j, d, item, valid, forward

    def ring_copy(dirn, j, d, item):
        return pltpu.make_async_remote_copy(kv.at[item, j], kv.at[item, j], ring_ssem.at[dirn, d - 1, j], ring_rsem.at[dirn, d - 1, j],
                                            device_id=device(neighbour(dirn), core))

    def poll_first(s):
        for dirn in range(2):
            j, d, item, valid, forward = event(s, dirn)

            @pl.when(valid)
            def _():
                for k in range(CORES):
                    pltpu.make_async_remote_copy(stage.at[0, 0], kv.at[item, j, k], first_ssem.at[0, 0, 0], first_rsem.at[dirn, j, k],
                                                 device_id={'sp': partner}).wait_recv()

            @pl.when(forward)
            def _():
                ring_copy(dirn, j, d, item).start()

    def poll(s):
        for dirn in range(2):
            j, d, item, valid, forward = event(s, dirn)

            @pl.when(valid)
            def _():
                ring_copy(dirn, j, d - 1, item).wait_recv()

            @pl.when(forward)
            def _():
                ring_copy(dirn, j, d, item).start()

    def drain(s):
        for dirn in range(2):
            j, d, item, valid, forward = event(s, dirn)

            @pl.when(forward)
            def _():
                ring_copy(dirn, j, d, item).wait_send()

    def project_q(idx, carry):
        slot = (idx + 4) % 3
        for copy in q_copies(idx):
            copy.wait()
        raw = dot(h_buf[...].reshape(chip_rows, dim), w_buf[slot])

        @pl.when(idx == 0)
        def _():
            for copy in q_copies(3):
                copy.start()

        @pl.when(idx > 0)
        def _():
            poll_first(idx - 1)

        for g in range(group):
            t = raw[:, g * head:(g + 1) * head].T
            t = t * lax.rsqrt(jnp.mean(t * t, axis=0, keepdims=True) + EPS) * gain_t[...]
            t1 = t[:half_head]
            t2 = t[half_head:]
            c = cos_t[...]
            s = sin_t[...]
            q_t[idx, :, g * chip_rows:(g + 1) * chip_rows] = jnp.concatenate([t1 * c - t2 * s, t2 * c + t1 * s], axis=0).astype(BF16)
        return carry

    lax.fori_loop(0, local_heads, project_q, 0)
    for b in range(wo_sem.shape[0]):
        wo_copy(b).start()

    score_scale = (head ** -0.5) * LOG2E

    def attend(item, j, first):
        keys = kv[item, j, :, 0].reshape(chip_rows, head)
        vals = jnp.concatenate([kv[item, j, 0, 1], kv[item, j, 1, 1]], axis=1)
        all_scores = [dot(keys, q_t[j, :, g * chip_rows:(g + 1) * chip_rows]) for g in range(group)]
        for g in range(group):
            cols = slice(g * chip_rows, (g + 1) * chip_rows)
            scores = all_scores[g]
            if first:
                key_pos = lax.broadcasted_iota(jnp.int32, scores.shape, 0)
                q_pos = lax.broadcasted_iota(jnp.int32, scores.shape, 1)
                scores = jnp.where(key_pos <= q_pos, scores, -jnp.inf)
                m_new = jnp.broadcast_to(jnp.max(scores, axis=0, keepdims=True), (8, chip_rows))
            else:
                m_old = m_buf[j, :, cols]
                m_new = jnp.maximum(m_old, jnp.max(scores, axis=0, keepdims=True))
            blocks = scores.reshape(chip_rows // 8, 8, chip_rows)
            prob = jnp.exp2((blocks - m_new[None]) * score_scale)
            total = jnp.sum(prob, axis=0)
            mixed = dot(vals, prob.reshape(chip_rows, chip_rows).astype(BF16))
            m_buf[j, :, cols] = m_new
            if first:
                l_buf[j, :, cols] = total
                o_t[j, :, cols] = mixed
            else:
                alpha = jnp.exp2((m_old - m_new) * score_scale)
                l_buf[j, :, cols] = l_buf[j, :, cols] * alpha + total
                old = o_t[j, :, cols].reshape(head // 8, 8, chip_rows)
                o_t[j, :, cols] = (old * alpha[None]).reshape(head, chip_rows) + mixed

    def diagonal(j, carry):
        pltpu.make_async_remote_copy(kv.at[chip, j, 0], kv.at[chip, j, 1 - core], d2d_ssem.at[j], d2d_rsem.at[j], device_id={'sp': partner}).wait_recv()
        attend(chip, j, True)
        return carry

    lax.fori_loop(0, local_heads, diagonal, 0)
    poll_first(local_heads - 1)

    def ring_step(s, carry):
        @pl.when(s >= local_heads)
        def _():
            poll(s)

        @pl.when(s >= DRAIN_LAG)
        def _():
            drain(s - DRAIN_LAG)

        def one(dirn, inner):
            up = event(s, 0)
            down = event(s, 1)
            j, item, valid = (jnp.where(dirn == 0, up[k], down[k]) for k in (0, 2, 3))

            @pl.when(valid & (item < chip))
            def _():
                attend(item, j, False)

            return inner

        lax.fori_loop(0, 2, one, 0)
        return carry

    def o_copy(j):
        cols = pl.ds(j * width, width)
        return pltpu.make_async_remote_copy(o_send.at[:, cols], o_all.at[core, :, cols], o_ssem.at[j], o_rsem.at[j], device_id={'sp': partner})

    def close_head(j):
        inv = 1.0 / jnp.sum(l_buf[j], axis=0, keepdims=True)
        for g in range(group):
            cols = slice(g * chip_rows, (g + 1) * chip_rows)
            o_val = (o_t[j, :, cols] * inv[:, cols]).T.astype(BF16)
            out_cols = slice(j * width + g * head, j * width + (g + 1) * head)
            o_all[core, :, out_cols] = jnp.where(core == 0, o_val[:rows], o_val[rows:])
            o_send[:, out_cols] = jnp.where(core == 0, o_val[rows:], o_val[:rows])
        o_copy(j).start()

    def out_copy(n):
        cols = pl.ds(n * width, width)
        return pltpu.make_async_copy(acc.at[:, cols], out_hbm.at[:, cols], out_sem.at[n])

    def project_out(first_head, last_head, start, end):
        for j in range(first_head, last_head):
            for c in range(CORES):
                wo_copy(c * local_heads + j).wait()
        for j in range(first_head, last_head):
            o_copy(j).wait_recv()
        depth = slice(first_head * width, last_head * width)

        def block(n, carry):
            cols = pl.ds(pl.multiple_of(n * width, width), width)
            total = x_buf[:, cols].astype(F32) if start else acc[:, cols]
            for c in range(CORES):
                total = total + dot(o_all[c, :, depth], wo_buf[c * mixed_dim + depth.start:c * mixed_dim + depth.stop, cols])
            acc[:, cols] = total
            if end:
                out_copy(n).start()
            return carry

        lax.fori_loop(0, dim // width, block, 0)

    lax.fori_loop(0, SLOTS - 2, ring_step, 0)
    close_head(0)
    close_head(1)
    lax.fori_loop(SLOTS - 2, SLOTS - 1, ring_step, 0)
    close_head(2)
    project_out(0, 2, True, False)
    lax.fori_loop(SLOTS - 1, SLOTS, ring_step, 0)
    close_head(3)
    project_out(2, 3, False, False)
    project_out(3, 4, False, True)

    h_copy.wait_send()
    for j in range(local_heads):
        o_copy(j).wait_send()

    def drain_first(idx, carry):
        for e in range(2):
            for copy, cond in first_copies(idx, e):
                pl.when(cond)(copy.wait_send)
        return carry

    lax.fori_loop(0, 4, drain_first, 0)
    for s in range(SLOTS - DRAIN_LAG, SLOTS):
        drain(s)
    for n in range(dim // width):
        out_copy(n).wait()


def solution(mesh):
    group_size = mesh.shape['sp']

    def device_step(hidden, ln_gain, w_q, w_k, w_v, w_o, q_gain, k_gain):
        rows, dim = hidden.shape
        head = q_gain.shape[0]
        half = head // 2
        chips = group_size // CORES
        local_heads = w_k.shape[1] // head // CORES
        width = w_q.shape[1] // CORES // local_heads
        chip_rows = rows * CORES
        inv_freq = THETA ** -(np.arange(half, dtype=np.float64) * (2.0 / head))
        angles = inv_freq[:, None] * np.arange(rows * group_size)[None, :]
        cos_all = jnp.asarray(np.cos(angles).astype(np.float32))
        sin_all = jnp.asarray(np.sin(angles).astype(np.float32))
        hbm = pl.BlockSpec(memory_space=pl.ANY)
        dma = pltpu.SemaphoreType.DMA
        wide = width // head * chip_rows
        total = pl.pallas_call(
            functools.partial(kernel, group_size),
            out_shape=jax.ShapeDtypeStruct((rows, dim), F32),
            in_specs=[hbm] * 10,
            out_specs=hbm,
            scratch_shapes=[
                pltpu.VMEM((rows, dim), BF16),
                pltpu.VMEM((CORES, rows, dim), BF16),
                pltpu.VMEM((3, dim, width), BF16),
                pltpu.VMEM(w_o.shape, BF16),
                pltpu.VMEM((chips, local_heads, CORES, 2, rows, head), BF16),
                pltpu.VMEM((4, 2, 2, rows, head), BF16),
                pltpu.VMEM((local_heads, head, wide), BF16),
                pltpu.VMEM((local_heads, head, wide), F32),
                pltpu.VMEM((local_heads, 8, wide), F32),
                pltpu.VMEM((local_heads, 8, wide), F32),
                pltpu.VMEM((CORES, rows, local_heads * width), BF16),
                pltpu.VMEM((rows, local_heads * width), BF16),
                pltpu.VMEM((rows, dim), F32),
                pltpu.VMEM((1, dim), BF16),
                pltpu.VMEM((2, 1, head), BF16),
                pltpu.VMEM((half, chip_rows), F32),
                pltpu.VMEM((half, chip_rows), F32),
                pltpu.VMEM((head, chip_rows), F32),
                pltpu.VMEM((rows, head), F32),
                pltpu.VMEM((rows, head), F32),
                dma((4,)), dma((5,)), dma((3, 2)), dma((w_o.shape[0] // width,)), dma, dma,
                dma((local_heads,)), dma((local_heads,)),
                dma((2, 4, 2)), dma((2, local_heads, CORES)),
                dma((2, chips // 2, local_heads)), dma((2, chips // 2, local_heads)),
                dma((local_heads,)), dma((local_heads,)), dma((dim // width,)),
            ],
            compiler_params=pltpu.CompilerParams(collective_id=0, has_side_effects=True, vmem_limit_bytes=67043328),
        )(hidden, w_q, w_k, w_v, w_o, ln_gain[None, :], q_gain[None, :], k_gain[None, :], cos_all, sin_all)
        return total.astype(BF16)

    row_spec = P(('dp', 'sp'), None)
    return jax.shard_map(device_step, mesh=mesh, in_specs=(row_spec, P(), P(), P(), P(), P(), P(), P()), out_specs=row_spec, check_vma=False)
```

time: 86.5 us -> 62.4 us (0.72)
  the two profiles are of different devices: /device:TPU:253 before, /device:TPU:244 now
where the time goes in v2:
time: 62.4 us; the launch traced here: 62.2 us
  Pallas kernels  58.1 us (93%)
  other arithmetic  2.69 us (4%)
  local copies, waits for them, and re-layouts  1.31 us (2%)
    pallas_call x1, Pallas kernels, device_step(): pl.pallas_call(functools.partial(kernel, group_size), out_shape=jax.Shape...  58.1 us
    convert_element_type x1, other arithmetic, device_step(): return total.astype(BF16)  2.69 us
    broadcast_in_dim x1, local copies, waits for them, and re-layouts, device_step(): ln_gain[None, :]  1.31 us

profile of v2, /device:TPU:244, one launch (start us, length us, event | category | flops | bytes accessed | tf_op | source)
XLA Modules:
  0.0 62.2 jit_solution(1652658072795661718)
XLA Ops:
  0.0 1.3 %broadcast_in_dim.9.ln_hbm = bf16[1,4096]{1,0:T(2,128)(2,1)} reshape(bf16[4096]{0:T(1024)(128)(2,1)} %param.11) | data formatting | bytes 16384 | tf_op jit(solution)/shard_map/broadcast_in_dim | solution.py:447
  1.3 58.1 %shard_map.100 = f32[128,4096]{1,0:T(8,128)} custom-call(bf16[128,4096]{1,0:T(8,128)(2,1)} %x_hbm.1, bf16[4096,4096]{1,0:T(8,128)(2,1)} %wq.1, bf16[4096,1024]{1,0:T(8,128)(2,1)} %wk.1, bf16[4096,1024]{1,0:T(8,128)(2,1)} %wv.1, bf16[4096,4096]{1,0:T(8,128)(2,1)} %wo.1, bf16[1,4096]{1,0:T(2,128)(2,1)} %broadcast_in_dim.9.ln_hbm, bf16[1,128]{1,0:T(2,128)(2,1)} %bitcast.2, ...), custom_call_target="tpu_custom_call" | custom-call | tf_op jit(solution)/shard_map/pallas_call | solution.py:414
  59.5 2.7 %convert_element_type.3 = bf16[128,4096]{1,0:T(8,128)(2,1)} convert(f32[128,4096]{1,0:T(8,128)} %shard_map.100) | non-fusion elementwise | flops 524288 | bytes 3145728 | tf_op jit(solution)/shard_map/convert_element_type | solution.py:448

commit v3 on v2

--- a/solution.py
+++ b/solution.py
@@ -11,6 +11,8 @@
 THETA = 1000000.0
 LOG2E = 1.4426950408889634
 CORES = 2
+LANES = 128
+VMEM_LIMIT = 62 * 2 ** 20
 BF16 = jnp.bfloat16
 F32 = jnp.float32
 
@@ -32,10 +34,10 @@
 DRAIN_LAG = 7
 
 
-def kernel(group_size, x_hbm, wq, wk, wv, wo, ln_hbm, q_gain_hbm, k_gain_hbm, cos_hbm, sin_hbm, out_hbm,
+def kernel(group_size, x_hbm, wq, wk, wv, wo, ln_hbm, q_gain_hbm, k_gain_hbm, cos_hbm, sin_hbm, out_ref,
            x_buf, h_buf, w_buf, wo_buf, kv, stage, q_t, o_t, m_buf, l_buf, o_all, o_send, acc,
            ln_buf, gain_buf, cos_t, sin_t, gain_t, cos_k, sin_k,
-           x_sem, small_sem, w_sem, wo_sem, h_ssem, h_rsem, d2d_ssem, d2d_rsem, first_ssem, first_rsem, ring_ssem, ring_rsem, o_ssem, o_rsem, out_sem):
+           x_sem, small_sem, w_sem, wo_sem, h_ssem, h_rsem, d2d_ssem, d2d_rsem, first_ssem, first_rsem, ring_ssem, ring_rsem, o_ssem, o_rsem):
     chips = group_size // CORES
     me = lax.axis_index('sp')
     chip = me // CORES
@@ -50,6 +52,7 @@
     chip_rows = rows * CORES
     far = chips // 2
     mixed_dim = local_heads * width
+    lanes = ln_buf.shape[1]
 
     def device(c, k):
         return {'sp': c * CORES + k}
@@ -114,7 +117,9 @@
             sl = slice(r * part_rows + t * step_rows, r * part_rows + (t + 1) * step_rows)
             xf = x_buf[sl, :].astype(F32)
             scale = lax.rsqrt(jnp.mean(xf * xf, axis=-1, keepdims=True) + EPS)
-            h_buf[core, sl, :] = (xf * scale * ln_buf[...].astype(F32)).astype(BF16)
+            for b in range(dim // lanes):
+                cols = slice(b * lanes, (b + 1) * lanes)
+                h_buf[core, sl, cols] = (xf[:, cols] * scale * ln_buf[b:b + 1, :].astype(F32)).astype(BF16)
 
     for copy in small[1:]:
         copy.wait()
@@ -199,7 +204,7 @@
         return j, d, item, valid, forward
 
     def ring_copy(dirn, j, d, item):
-        return pltpu.make_async_remote_copy(kv.at[item, j], kv.at[item, j], ring_ssem.at[dirn, d - 1, j], ring_rsem.at[dirn, d - 1, j],
+        return pltpu.make_async_remote_copy(kv.at[item, j], kv.at[item, j], ring_ssem.at[dirn, (d - 1) * local_heads + j], ring_rsem.at[dirn, (d - 1) * local_heads + j],
                                             device_id=device(neighbour(dirn), core))
 
     def poll_first(s):
@@ -341,10 +346,6 @@
             o_send[:, out_cols] = jnp.where(core == 0, o_val[rows:], o_val[:rows])
         o_copy(j).start()
 
-    def out_copy(n):
-        cols = pl.ds(n * width, width)
-        return pltpu.make_async_copy(acc.at[:, cols], out_hbm.at[:, cols], out_sem.at[n])
-
     def project_out(first_head, last_head, start, end):
         for j in range(first_head, last_head):
             for c in range(CORES):
@@ -354,16 +355,19 @@
         depth = slice(first_head * width, last_head * width)
 
         def block(n, carry):
-            cols = pl.ds(pl.multiple_of(n * width, width), width)
-            total = x_buf[:, cols].astype(F32) if start else acc[:, cols]
-            for c in range(CORES):
-                total = total + dot(o_all[c, :, depth], wo_buf[c * mixed_dim + depth.start:c * mixed_dim + depth.stop, cols])
-            acc[:, cols] = total
-            if end:
-                out_copy(n).start()
+            for w in range(wide // width):
+                cols = pl.ds(pl.multiple_of(n * wide + w * width, width), width)
+                total = x_buf[:, cols].astype(F32) if start else acc[:, cols]
+                for c in range(CORES):
+                    total = total + dot(o_all[c, :, depth], wo_buf[c * mixed_dim + depth.start:c * mixed_dim + depth.stop, cols])
+                if end:
+                    out_ref[:, cols] = total.astype(BF16)
+                else:
+                    acc[:, cols] = total
             return carry
 
-        lax.fori_loop(0, dim // width, block, 0)
+        wide = dim // 2
+        lax.fori_loop(0, dim // wide, block, 0)
 
     lax.fori_loop(0, SLOTS - 2, ring_step, 0)
     close_head(0)
@@ -389,8 +393,6 @@
     lax.fori_loop(0, 4, drain_first, 0)
     for s in range(SLOTS - DRAIN_LAG, SLOTS):
         drain(s)
-    for n in range(dim // width):
-        out_copy(n).wait()
 
 
 def solution(mesh):
@@ -411,11 +413,11 @@
         hbm = pl.BlockSpec(memory_space=pl.ANY)
         dma = pltpu.SemaphoreType.DMA
         wide = width // head * chip_rows
-        total = pl.pallas_call(
+        return pl.pallas_call(
             functools.partial(kernel, group_size),
-            out_shape=jax.ShapeDtypeStruct((rows, dim), F32),
+            out_shape=pltpu.VMEM((rows, dim), BF16),
             in_specs=[hbm] * 10,
-            out_specs=hbm,
+            out_specs=pl.BlockSpec(memory_space=pltpu.VMEM),
             scratch_shapes=[
                 pltpu.VMEM((rows, dim), BF16),
                 pltpu.VMEM((CORES, rows, dim), BF16),
@@ -430,22 +432,21 @@
                 pltpu.VMEM((CORES, rows, local_heads * width), BF16),
                 pltpu.VMEM((rows, local_heads * width), BF16),
                 pltpu.VMEM((rows, dim), F32),
-                pltpu.VMEM((1, dim), BF16),
+                pltpu.VMEM((dim // LANES, LANES), BF16),
                 pltpu.VMEM((2, 1, head), BF16),
                 pltpu.VMEM((half, chip_rows), F32),
                 pltpu.VMEM((half, chip_rows), F32),
                 pltpu.VMEM((head, chip_rows), F32),
                 pltpu.VMEM((rows, head), F32),
                 pltpu.VMEM((rows, head), F32),
-                dma((4,)), dma((5,)), dma((3, 2)), dma((w_o.shape[0] // width,)), dma, dma,
+                dma((2,)), dma((5,)), dma((3, 2)), dma((w_o.shape[0] // width,)), dma, dma,
                 dma((local_heads,)), dma((local_heads,)),
                 dma((2, 4, 2)), dma((2, local_heads, CORES)),
-                dma((2, chips // 2, local_heads)), dma((2, chips // 2, local_heads)),
-                dma((local_heads,)), dma((local_heads,)), dma((dim // width,)),
+                dma((2, (chips // 2 - 1) * local_heads)), dma((2, (chips // 2 - 1) * local_heads)),
+                dma((local_heads,)), dma((local_heads,)),
             ],
-            compiler_params=pltpu.CompilerParams(collective_id=0, has_side_effects=True, vmem_limit_bytes=67043328),
-        )(hidden, w_q, w_k, w_v, w_o, ln_gain[None, :], q_gain[None, :], k_gain[None, :], cos_all, sin_all)
-        return total.astype(BF16)
+            compiler_params=pltpu.CompilerParams(collective_id=0, has_side_effects=True, vmem_limit_bytes=VMEM_LIMIT),
+        )(hidden, w_q, w_k, w_v, w_o, ln_gain.reshape(-1, LANES), q_gain[None, :], k_gain[None, :], cos_all, sin_all)
 
     row_spec = P(('dp', 'sp'), None)
     return jax.shard_map(device_step, mesh=mesh, in_specs=(row_spec, P(), P(), P(), P(), P(), P(), P()), out_specs=row_spec, check_vma=False)

time: 62.4 us -> 55.2 us (0.88)
  the two profiles are of different devices: /device:TPU:244 before, /device:TPU:214 now
where the time goes in v3:
time: 55.2 us; the launch traced here: 55 us
  Pallas kernels  54 us (98%)
  local copies, waits for them, and re-layouts  0.97 us (2%)
    pallas_call x1, Pallas kernels, device_step(): pl.pallas_call(functools.partial(kernel, group_size), out_shape=pltpu.VME...  54 us

profile of v3, /device:TPU:214, one launch (start us, length us, event | category | flops | bytes accessed | tf_op | source)
XLA Modules:
  0.0 55.0 jit_solution(18160828670844114106)
XLA Ops:
  0.0 54.0 %shard_map.100 = bf16[128,4096]{1,0:T(8,128)(2,1)S(1)} custom-call(bf16[128,4096]{1,0:T(8,128)(2,1)} %x_hbm.1, bf16[4096,4096]{1,0:T(8,128)(2,1)} %wq.1, bf16[4096,1024]{1,0:T(8,128)(2,1)} %wk.1, bf16[4096,1024]{1,0:T(8,128)(2,1)} %wv.1, bf16[4096,4096]{1,0:T(8,128)(2,1)} %wo.1, bf16[32,128]{1,0:T(8,128)(2,1)} %bitcast.3, bf16[1,128]{1,0:T(2,128)(2,1)} %bitcast.4, ...), custom_call_target="tpu_custom_call" | custom-call | tf_op jit(solution)/shard_map/pallas_call | solution.py:416
  54.1 1.0 %copy.12 = bf16[128,4096]{1,0:T(8,128)(2,1)} copy(bf16[128,4096]{1,0:T(8,128)(2,1)S(1)} %shard_map.100) | data formatting | bytes 2097152

commit v4 on v3

v4 whole, which is shorter than its diff:
```python
import functools
import jax
import jax.numpy as jnp
import numpy as np
from jax import lax
from jax.experimental import pallas as pl
from jax.experimental.pallas import tpu as pltpu
from jax.sharding import PartitionSpec as P

EPS = 1e-6
THETA = 1000000.0
LOG2E = 1.4426950408889634
CORES = 2
LANES = 128
VMEM_LIMIT = 62 * 2 ** 20
BF16 = jnp.bfloat16
F32 = jnp.float32


def dot(a, b):
    return jnp.dot(a, b, preferred_element_type=F32)


ORDER = ((0, 1), (1, 1), (2, 1), (3, 1), (0, 2), (1, 2), (0, 3), (1, 3), (2, 2), (0, 4), (1, 4), (3, 2), (2, 3), (3, 3), (2, 4), (3, 4))
SLOTS = len(ORDER)
EARLY = 2
EARLY_CLOSE = 10
EARLY_OUT = 11
THIRD_CLOSE = 14
DEFERRED = ((5, 2), (7, 3))


def slot_table(values):
    return tuple(sum(v << (2 * s) for s, v in enumerate(values[h:h + 8])) for h in (0, 8))


HEAD_TABLE = slot_table([j for j, _ in ORDER])
HOP_TABLE = slot_table([d - 1 for _, d in ORDER])


def lookup(table, s):
    return lax.shift_right_logical(jnp.where(s < 8, table[0], table[1]), 2 * (s % 8)) % 4


def kernel(group_size, x_hbm, wq, wk, wv, wo, ln_hbm, q_gain_hbm, k_gain_hbm, angle_hbm, out_ref,
           x_buf, h_buf, w_buf, wo_buf, kv, stage, q_t, o_t, m_buf, l_buf, o_all, o_send, acc,
           ln_buf, gain_buf, angle_t, gain_t, cos_k, sin_k,
           x_sem, small_sem, w_sem, wo_sem, h_ssem, h_rsem, d2d_ssem, d2d_rsem, first_ssem, first_rsem, ring_ssem, ring_rsem, o_ssem, o_rsem):
    chips = group_size // CORES
    me = lax.axis_index('sp')
    chip = me // CORES
    core = me % CORES
    partner = chip * CORES + (1 - core)
    rows, dim = x_buf.shape
    head = gain_buf.shape[2]
    half_head = head // 2
    width = w_buf.shape[2]
    local_heads = kv.shape[1]
    group = width // head
    chip_rows = rows * CORES
    far = chips // 2
    mixed_dim = local_heads * width
    lanes = ln_buf.shape[1]

    def device(c, k):
        return {'sp': c * CORES + k}

    def neighbour(dirn):
        return (chip + chips + 1 - 2 * dirn) % chips

    x_parts = x_sem.shape[0]
    part_rows = rows // x_parts

    def x_copy(r):
        sl = pl.ds(r * part_rows, part_rows)
        return pltpu.make_async_copy(x_hbm.at[sl, :], x_buf.at[sl, :], x_sem.at[r])

    chip_cols = pl.ds(pl.multiple_of(chip * chip_rows, chip_rows), chip_rows)
    small = (pltpu.make_async_copy(ln_hbm, ln_buf, small_sem.at[0]),
             pltpu.make_async_copy(q_gain_hbm, gain_buf.at[0], small_sem.at[1]),
             pltpu.make_async_copy(k_gain_hbm, gain_buf.at[1], small_sem.at[2]),
             pltpu.make_async_copy(angle_hbm.at[:, :, chip_cols], angle_t, small_sem.at[3]))

    def kv_copies(idx):
        pair = (idx % 2) * 2 + idx // 2
        cols = pl.ds(pl.multiple_of(pair * (width // 2), width // 2), width // 2)
        slot = idx % 3
        return (pltpu.make_async_copy(wk.at[:, cols], w_buf.at[slot, :, pl.ds(0, width // 2)], w_sem.at[slot]),
                pltpu.make_async_copy(wv.at[:, cols], w_buf.at[slot, :, pl.ds(width // 2, width // 2)], w_sem.at[slot]))

    def q_copies(idx):
        cols = pl.ds(pl.multiple_of((core * local_heads + idx) * width, width), width)
        slot = (idx + 4) % 3
        return tuple(pltpu.make_async_copy(wq.at[pl.ds(r * (dim // 2), dim // 2), cols],
                                           w_buf.at[slot, pl.ds(r * (dim // 2), dim // 2), :], w_sem.at[slot]) for r in range(2))

    def w_wait(slot):
        pltpu.make_async_copy(wq.at[:, pl.ds(0, width)], w_buf.at[slot], w_sem.at[slot]).wait()

    stages = ((0, EARLY), (EARLY, EARLY + 1), (EARLY + 1, local_heads))

    def wo_copies(k):
        first, last = stages[k]
        spans = [pl.ds(c * mixed_dim + first * width, (last - first) * width) for c in range(CORES)]
        return [pltpu.make_async_copy(wo.at[span, :], wo_buf.at[span, :], wo_sem.at[k]) for span in spans]

    def wo_wait(k):
        span = pl.ds(0, CORES * (stages[k][1] - stages[k][0]) * width)
        pltpu.make_async_copy(wo.at[span, :], wo_buf.at[span, :], wo_sem.at[k]).wait()

    for copy in small[:1]:
        copy.start()
    for r in range(x_parts):
        x_copy(r).start()
    for copy in small[1:]:
        copy.start()
    for copy in kv_copies(0):
        copy.start()

    barrier = pltpu.get_barrier_semaphore()
    pl.semaphore_signal(barrier, inc=1, device_id={'sp': partner})
    for dirn in range(2):
        for k in range(CORES):
            pl.semaphore_signal(barrier, inc=1, device_id=device(neighbour(dirn), k))

    small[0].wait()
    for r in range(x_parts):
        x_copy(r).wait()
        if r == x_parts - 1:
            for idx in range(1, 3):
                for copy in kv_copies(idx):
                    copy.start()
        step_rows = 16
        for t in range(part_rows // step_rows):
            sl = slice(r * part_rows + t * step_rows, r * part_rows + (t + 1) * step_rows)
            xf = x_buf[sl, :].astype(F32)
            scale = lax.rsqrt(jnp.mean(xf * xf, axis=-1, keepdims=True) + EPS)
            for b in range(dim // lanes):
                cols = slice(b * lanes, (b + 1) * lanes)
                h_buf[core, sl, cols] = (xf[:, cols] * scale * ln_buf[b:b + 1, :].astype(F32)).astype(BF16)

    for copy in small[1:]:
        copy.wait()
    gain_t[...] = jnp.broadcast_to(gain_buf[0].astype(F32), (chip_rows, head)).T
    own_cols = pl.ds(pl.multiple_of(core * rows, rows), rows)
    cos_own = angle_t[0, :, own_cols].T
    sin_own = angle_t[1, :, own_cols].T
    cos_k[...] = jnp.concatenate([cos_own, cos_own], axis=1)
    sin_k[...] = jnp.concatenate([-sin_own, sin_own], axis=1)

    pl.semaphore_wait(barrier, 1 + 2 * CORES)
    h_copy = pltpu.make_async_remote_copy(h_buf.at[core], h_buf.at[core], h_ssem, h_rsem, device_id={'sp': partner})

    def first_copies(idx):
        owner = idx % 2
        pair = idx // 2
        src = stage.at[idx]
        dst = kv.at[chip, pl.ds(pair * 2, 2), core]
        up = pltpu.make_async_remote_copy(src, dst, first_ssem.at[0, idx], first_rsem.at[0, pair, core], device_id=device(neighbour(0), owner))
        down = pltpu.make_async_remote_copy(src, dst, first_ssem.at[1, idx], first_rsem.at[1, pair, core], device_id=device(neighbour(1), owner))
        across = pltpu.make_async_remote_copy(src, dst, d2d_ssem.at[pair], d2d_rsem.at[pair], device_id={'sp': partner})
        return ((up, chip < chips - 1), (down, chip < far), (across, owner != core))

    def project_kv(idx, carry):
        slot = idx % 3
        w_wait(slot)
        raw = dot(h_buf[core], w_buf[slot])

        @pl.when(idx == 0)
        def _():
            for copy in kv_copies(3):
                copy.start()

        @pl.when(idx > 0)
        def _():
            for copy in q_copies(idx - 1):
                copy.start()

        for e in range(2):
            t = raw[:, e * head:(e + 1) * head]
            t = t * lax.rsqrt(jnp.mean(t * t, axis=-1, keepdims=True) + EPS) * gain_buf[1].astype(F32)
            k_val = (t * cos_k[...] + pltpu.roll(t, half_head, 1) * sin_k[...]).astype(BF16)
            v_val = raw[:, width // 2 + e * head:width // 2 + (e + 1) * head].T.astype(BF16)
            stage[idx, e, 0] = k_val
            stage[idx, e, 1] = v_val

            @pl.when(idx % 2 == core)
            def _():
                kv[chip, (idx // 2) * 2 + e, core, 0] = k_val
                kv[chip, (idx // 2) * 2 + e, core, 1] = v_val

        for copy, cond in first_copies(idx):
            pl.when(cond)(copy.start)

        @pl.when(idx == 0)
        def _():
            h_copy.start()

        return carry

    lax.fori_loop(0, 4, project_kv, 0)
    h_copy.wait_recv()

    def item_of(dirn, d):
        return (chip + chips + (2 * dirn - 1) * d) % chips

    def arrives(dirn, d):
        return chip >= d if dirn == 0 else item_of(1, d) < far

    def goes_on(dirn, d):
        return arrives(dirn, d) & (chip < chips - 1) if dirn == 0 else arrives(dirn, d)

    def ring_copy(dirn, j, d, whole):
        item = item_of(dirn, d - 1)
        sem = (d - 2) * local_heads + j
        ref = kv.at[item, j] if whole else kv.at[item, j, dirn]
        return pltpu.make_async_remote_copy(ref, ref, ring_ssem.at[dirn, sem], ring_rsem.at[dirn, sem], device_id=device(neighbour(dirn), core))

    def landed(dirn, j, d, whole):
        item = item_of(dirn, d)
        sem = (d - 2) * local_heads + j
        ref = kv.at[item, j] if whole else kv.at[item, j, dirn]
        return pltpu.make_async_remote_copy(ref, ref, ring_ssem.at[dirn, sem], ring_rsem.at[dirn, sem], device_id=device(neighbour(dirn), core))

    def forward_first(j):
        for dirn in range(2):
            pl.when(goes_on(dirn, 1))(ring_copy(dirn, j, 2, True).start)

    def poll_first(pair):
        for dirn in range(2):
            @pl.when(arrives(dirn, 1))
            def _():
                for k in range(CORES):
                    pltpu.make_async_remote_copy(stage.at[0], kv.at[item_of(dirn, 1), pl.ds(pair * 2, 2), k], first_ssem.at[0, 0],
                                                 first_rsem.at[dirn, pair, k], device_id={'sp': partner}).wait_recv()

    def poll(s):
        j = lookup(HEAD_TABLE, s)
        d = lookup(HOP_TABLE, s) + 1
        for dirn in range(2):
            pl.when(arrives(dirn, d) & (d < far))(landed(dirn, j, d, True).wait_recv)
            pl.when(arrives(dirn, d) & (d == far))(landed(dirn, j, d, False).wait_recv)
            pl.when(goes_on(dirn, d) & (d + 1 < far))(ring_copy(dirn, j, d + 1, True).start)
            pl.when(goes_on(dirn, d) & (d + 1 == far))(ring_copy(dirn, j, d + 1, False).start)

    def drain(j, carry):
        for d in range(1, far):
            for dirn in range(2):
                pl.when(goes_on(dirn, d))(ring_copy(dirn, j, d + 1, d + 1 < far).wait_send)
        return carry

    def project_q(idx, carry):
        slot = (idx + 4) % 3
        w_wait(slot)
        raw = dot(h_buf[...].reshape(chip_rows, dim), w_buf[slot])

        @pl.when(idx == 0)
        def _():
            for copy in q_copies(3):
                copy.start()

        @pl.when(idx == local_heads - 1)
        def _():
            poll_first(0)
            forward_first(0)
            forward_first(1)

        for g in range(group):
            t = raw[:, g * head:(g + 1) * head].T
            t = t * lax.rsqrt(jnp.mean(t * t, axis=0, keepdims=True) + EPS) * gain_t[...]
            t1 = t[:half_head]
            t2 = t[half_head:]
            c = angle_t[0]
            s = angle_t[1]
            q_t[idx, :, g * chip_rows:(g + 1) * chip_rows] = jnp.concatenate([t1 * c - t2 * s, t2 * c + t1 * s], axis=0).astype(BF16)
        return carry

    lax.fori_loop(0, local_heads, project_q, 0)
    for k in range(len(stages)):
        for copy in wo_copies(k):
            copy.start()

    score_scale = (head ** -0.5) * LOG2E

    def attend(items, j, first=False, ahead=2):
        keys = [kv[item, j, :, 0].reshape(chip_rows, head) for item in items]
        vals = jnp.concatenate([kv[item, j, c, 1] for item in items for c in range(CORES)], axis=1)

        def scores_of(g):
            return [dot(k, q_t[j, :, g * chip_rows:(g + 1) * chip_rows]) for k in keys]

        pending = [scores_of(g) for g in range(ahead)]
        for g in range(group):
            cols = slice(g * chip_rows, (g + 1) * chip_rows)
            scores = pending[g]
            if first:
                key_pos = lax.broadcasted_iota(jnp.int32, scores[0].shape, 0)
                q_pos = lax.broadcasted_iota(jnp.int32, scores[0].shape, 1)
                scores = [jnp.where(key_pos <= q_pos, scores[0], -jnp.inf)]
            top = functools.reduce(jnp.maximum, [jnp.max(x.reshape(chip_rows // 8, 8, chip_rows), axis=0) for x in scores])
            top = jnp.max(top, axis=0, keepdims=True)
            if first:
                m_new = jnp.broadcast_to(top, (8, chip_rows))
            else:
                m_old = m_buf[j, :, cols]
                m_new = jnp.maximum(m_old, top)
            probs = [jnp.exp2((x.reshape(chip_rows // 8, 8, chip_rows) - m_new[None]) * score_scale) for x in scores]
            total = functools.reduce(jnp.add, [jnp.sum(p, axis=0) for p in probs])
            if g + ahead < group:
                pending.append(scores_of(g + ahead))
            mixed = dot(vals, jnp.concatenate([p.reshape(chip_rows, chip_rows).astype(BF16) for p in probs], axis=0))
            m_buf[j, :, cols] = m_new
            if first:
                l_buf[j, :, cols] = total
                o_t[j, :, cols] = mixed
            else:
                alpha = jnp.exp2((m_old - m_new) * score_scale)
                l_buf[j, :, cols] = l_buf[j, :, cols] * alpha + total
                old = o_t[j, :, cols].reshape(head // 8, 8, chip_rows)
                o_t[j, :, cols] = (old * alpha[None]).reshape(head, chip_rows) + mixed

    def diagonal(j, carry):
        @pl.when(j % 2 == 0)
        def _():
            pltpu.make_async_remote_copy(stage.at[0], kv.at[chip, pl.ds(j, 2), 1 - core], d2d_ssem.at[j // 2], d2d_rsem.at[j // 2],
                                         device_id={'sp': partner}).wait_recv()

        attend((chip,), j, first=True, ahead=group)
        return carry

    lax.fori_loop(0, local_heads, diagonal, 0)
    poll_first(1)

    def o_copy(k):
        cols = pl.ds(stages[k][0] * width, (stages[k][1] - stages[k][0]) * width)
        return pltpu.make_async_remote_copy(o_send.at[:, cols], o_all.at[core, :, cols], o_ssem.at[k], o_rsem.at[k], device_id={'sp': partner})

    def close_head(j):
        inv = 1.0 / jnp.sum(l_buf[j], axis=0, keepdims=True)
        for g in range(group):
            cols = slice(g * chip_rows, (g + 1) * chip_rows)
            o_val = (o_t[j, :, cols] * inv[:, cols]).T.astype(BF16)
            out_cols = slice(j * width + g * head, j * width + (g + 1) * head)
            o_all[core, :, out_cols] = jnp.where(core == 0, o_val[:rows], o_val[rows:])
            o_send[:, out_cols] = jnp.where(core == 0, o_val[rows:], o_val[:rows])

    def project_out(k, start, end):
        first_head, last_head = stages[k]
        wo_wait(k)
        o_copy(k).wait_recv()
        depth = slice(first_head * width, last_head * width)

        def block(n, carry):
            for w in range(wide // width):
                cols = pl.ds(pl.multiple_of(n * wide + w * width, width), width)
                total = x_buf[:, cols].astype(F32) if start else acc[:, cols]
                for c in range(CORES):
                    total = total + dot(o_all[c, :, depth], wo_buf[c * mixed_dim + depth.start:c * mixed_dim + depth.stop, cols])
                if end:
                    out_ref[:, cols] = total.astype(BF16)
                else:
                    acc[:, cols] = total
            return carry

        wide = dim // 2
        lax.fori_loop(0, dim // wide, block, 0)

    def ring_step(s, carry):
        @pl.when(s >= local_heads)
        def _():
            poll(s)

        for at, j in DEFERRED:
            @pl.when(s == at)
            def _():
                forward_first(j)

        j = lookup(HEAD_TABLE, s)
        d = lookup(HOP_TABLE, s) + 1
        both = (d < far) & (chip + d >= chips)

        @pl.when(both)
        def _():
            attend((item_of(0, d), item_of(1, d)), j)

        @pl.when((chip >= d) & jnp.logical_not(both))
        def _():
            attend((item_of(0, d),), j, ahead=group)

        @pl.when(s == EARLY_CLOSE)
        def _():
            for early in range(EARLY):
                close_head(early)
            o_copy(0).start()

        @pl.when(s == EARLY_OUT)
        def _():
            project_out(0, True, False)

        @pl.when(s == THIRD_CLOSE)
        def _():
            close_head(EARLY)
            o_copy(1).start()

        return carry

    lax.fori_loop(0, SLOTS, ring_step, 0)
    close_head(local_heads - 1)
    o_copy(2).start()
    project_out(1, False, False)
    project_out(2, False, True)

    h_copy.wait_send()
    for k in range(len(stages)):
        o_copy(k).wait_send()

    def drain_first(idx, carry):
        for copy, cond in first_copies(idx):
            pl.when(cond)(copy.wait_send)
        return carry

    lax.fori_loop(0, 4, drain_first, 0)
    lax.fori_loop(0, local_heads, drain, 0)


def solution(mesh):
    group_size = mesh.shape['sp']

    def device_step(hidden, ln_gain, w_q, w_k, w_v, w_o, q_gain, k_gain):
        rows, dim = hidden.shape
        head = q_gain.shape[0]
        half = head // 2
        chips = group_size // CORES
        local_heads = w_k.shape[1] // head // CORES
        width = w_q.shape[1] // CORES // local_heads
        chip_rows = rows * CORES
        inv_freq = THETA ** -(np.arange(half, dtype=np.float64) * (2.0 / head))
        angles = inv_freq[:, None] * np.arange(rows * group_size)[None, :]
        angle_all = jnp.asarray(np.stack([np.cos(angles), np.sin(angles)]).astype(np.float32))
        hbm = pl.BlockSpec(memory_space=pl.ANY)
        dma = pltpu.SemaphoreType.DMA
        wide = width // head * chip_rows
        return pl.pallas_call(
            functools.partial(kernel, group_size),
            out_shape=pltpu.VMEM((rows, dim), BF16),
            in_specs=[hbm] * 9,
            out_specs=pl.BlockSpec(memory_space=pltpu.VMEM),
            scratch_shapes=[
                pltpu.VMEM((rows, dim), BF16),
                pltpu.VMEM((CORES, rows, dim), BF16),
                pltpu.VMEM((3, dim, width), BF16),
                pltpu.VMEM(w_o.shape, BF16),
                pltpu.VMEM((chips, local_heads, CORES, 2, rows, head), BF16),
                pltpu.VMEM((4, 2, 2, rows, head), BF16),
                pltpu.VMEM((local_heads, head, wide), BF16),
                pltpu.VMEM((local_heads, head, wide), F32),
                pltpu.VMEM((local_heads, 8, wide), F32),
                pltpu.VMEM((local_heads, 8, wide), F32),
                pltpu.VMEM((CORES, rows, local_heads * width), BF16),
                pltpu.VMEM((rows, local_heads * width), BF16),
                pltpu.VMEM((rows, dim), F32),
                pltpu.VMEM((dim // LANES, LANES), BF16),
                pltpu.VMEM((2, 1, head), BF16),
                pltpu.VMEM((2, half, chip_rows), F32),
                pltpu.VMEM((head, chip_rows), F32),
                pltpu.VMEM((rows, head), F32),
                pltpu.VMEM((rows, head), F32),
                dma((2,)), dma((4,)), dma((3,)), dma((3,)), dma, dma,
                dma((2,)), dma((2,)),
                dma((2, 4)), dma((2, 2, CORES)),
                dma((2, (chips // 2 - 1) * local_heads)), dma((2, (chips // 2 - 1) * local_heads)),
                dma((3,)), dma((3,)),
            ],
            compiler_params=pltpu.CompilerParams(collective_id=0, has_side_effects=True, vmem_limit_bytes=VMEM_LIMIT),
        )(hidden, w_q, w_k, w_v, w_o, ln_gain.reshape(-1, LANES), q_gain[None, :], k_gain[None, :], angle_all)

    row_spec = P(('dp', 'sp'), None)
    return jax.shard_map(device_step, mesh=mesh, in_specs=(row_spec, P(), P(), P(), P(), P(), P(), P()), out_specs=row_spec, check_vma=False)
```

time: 55.2 us -> 52.7 us (0.955)
  the two profiles are of different devices: /device:TPU:214 before, /device:TPU:182 now
where the time goes in v4:
time: 52.7 us; the launch traced here: 52.6 us
  Pallas kernels  51.6 us (98%)
  local copies, waits for them, and re-layouts  0.97 us (2%)
    pallas_call x1, Pallas kernels, device_step(): pl.pallas_call(functools.partial(kernel, group_size), out_shape=pltpu.VME...  51.6 us

profile of v4, /device:TPU:182, one launch (start us, length us, event | category | flops | bytes accessed | tf_op | source)
XLA Modules:
  0.0 52.6 jit_solution(1106482015709660009)
XLA Ops:
  0.0 51.6 %shard_map.91 = bf16[128,4096]{1,0:T(8,128)(2,1)S(1)} custom-call(bf16[128,4096]{1,0:T(8,128)(2,1)} %x_hbm.1, bf16[4096,4096]{1,0:T(8,128)(2,1)} %wq.1, bf16[4096,1024]{1,0:T(8,128)(2,1)} %wk.1, bf16[4096,1024]{1,0:T(8,128)(2,1)} %wv.1, bf16[4096,4096]{1,0:T(8,128)(2,1)} %wo.1, bf16[32,128]{1,0:T(8,128)(2,1)} %bitcast.3, bf16[1,128]{1,0:T(2,128)(2,1)} %bitcast.4, ...), custom_call_target="tpu_custom_call" | custom-call | tf_op jit(solution)/shard_map/pallas_call | solution.py:443
  51.6 1.0 %copy.11 = bf16[128,4096]{1,0:T(8,128)(2,1)} copy(bf16[128,4096]{1,0:T(8,128)(2,1)S(1)} %shard_map.91) | data formatting | bytes 2097152

commit v5 on v4

--- a/solution.py
+++ b/solution.py
@@ -28,6 +28,7 @@
 EARLY_OUT = 11
 THIRD_CLOSE = 14
 DEFERRED = ((5, 2), (7, 3))
+NEAR, REST, WHOLE = 0, 1, 2
 
 
 def slot_table(values):
@@ -85,27 +86,32 @@
         pair = (idx % 2) * 2 + idx // 2
         cols = pl.ds(pl.multiple_of(pair * (width // 2), width // 2), width // 2)
         slot = idx % 3
-        return (pltpu.make_async_copy(wk.at[:, cols], w_buf.at[slot, :, pl.ds(0, width // 2)], w_sem.at[slot]),
-                pltpu.make_async_copy(wv.at[:, cols], w_buf.at[slot, :, pl.ds(width // 2, width // 2)], w_sem.at[slot]))
+        return (pltpu.make_async_copy(wk.at[:, cols], w_buf.at[slot, :, pl.ds(0, width // 2)], w_sem.at[slot, 0]),
+                pltpu.make_async_copy(wv.at[:, cols], w_buf.at[slot, :, pl.ds(width // 2, width // 2)], w_sem.at[slot, 1]))
 
     def q_copies(idx):
         cols = pl.ds(pl.multiple_of((core * local_heads + idx) * width, width), width)
         slot = (idx + 4) % 3
         return tuple(pltpu.make_async_copy(wq.at[pl.ds(r * (dim // 2), dim // 2), cols],
-                                           w_buf.at[slot, pl.ds(r * (dim // 2), dim // 2), :], w_sem.at[slot]) for r in range(2))
-
-    def w_wait(slot):
-        pltpu.make_async_copy(wq.at[:, pl.ds(0, width)], w_buf.at[slot], w_sem.at[slot]).wait()
+                                           w_buf.at[slot, pl.ds(r * (dim // 2), dim // 2), :], w_sem.at[slot, r]) for r in range(2))
 
     stages = ((0, EARLY), (EARLY, EARLY + 1), (EARLY + 1, local_heads))
 
+    def span_of(k, c):
+        first, last = stages[k]
+        return (CORES * first + c * (last - first)) * width, (last - first) * width
+
     def wo_copies(k):
-        first, last = stages[k]
-        spans = [pl.ds(c * mixed_dim + first * width, (last - first) * width) for c in range(CORES)]
-        return [pltpu.make_async_copy(wo.at[span, :], wo_buf.at[span, :], wo_sem.at[k]) for span in spans]
+        copies = []
+        for c in range(CORES):
+            at, size = span_of(k, c)
+            source = pl.ds(c * mixed_dim + stages[k][0] * width, size)
+            copies.append(pltpu.make_async_copy(wo.at[source, :], wo_buf.at[pl.ds(at, size), :], wo_sem.at[k]))
+        return copies
 
     def wo_wait(k):
-        span = pl.ds(0, CORES * (stages[k][1] - stages[k][0]) * width)
+        at, size = span_of(k, 0)
+        span = pl.ds(at, CORES * size)
         pltpu.make_async_copy(wo.at[span, :], wo_buf.at[span, :], wo_sem.at[k]).wait()
 
     for copy in small[:1]:
@@ -114,8 +120,7 @@
         x_copy(r).start()
     for copy in small[1:]:
         copy.start()
-    for copy in kv_copies(0):
-        copy.start()
+    kv_copies(0)[0].start()
 
     barrier = pltpu.get_barrier_semaphore()
     pl.semaphore_signal(barrier, inc=1, device_id={'sp': partner})
@@ -126,6 +131,8 @@
     small[0].wait()
     for r in range(x_parts):
         x_copy(r).wait()
+        if r == 0:
+            kv_copies(0)[1].start()
         if r == x_parts - 1:
             for idx in range(1, 3):
                 for copy in kv_copies(idx):
@@ -141,7 +148,6 @@
 
     for copy in small[1:]:
         copy.wait()
-    gain_t[...] = jnp.broadcast_to(gain_buf[0].astype(F32), (chip_rows, head)).T
     own_cols = pl.ds(pl.multiple_of(core * rows, rows), rows)
     cos_own = angle_t[0, :, own_cols].T
     sin_own = angle_t[1, :, own_cols].T
@@ -163,8 +169,12 @@
 
     def project_kv(idx, carry):
         slot = idx % 3
-        w_wait(slot)
-        raw = dot(h_buf[core], w_buf[slot])
+        raws = []
+        for part, copy in enumerate(kv_copies(idx)):
+            copy.wait()
+            cols = slice(part * (width // 2), (part + 1) * (width // 2))
+            raws.append(dot(h_buf[core, :, :dim // 2], w_buf[slot, :dim // 2, cols]) + dot(h_buf[core, :, dim // 2:], w_buf[slot, dim // 2:, cols]))
+        k_raw, v_raw = raws
 
         @pl.when(idx == 0)
         def _():
@@ -177,10 +187,10 @@
                 copy.start()
 
         for e in range(2):
-            t = raw[:, e * head:(e + 1) * head]
+            t = k_raw[:, e * head:(e + 1) * head]
             t = t * lax.rsqrt(jnp.mean(t * t, axis=-1, keepdims=True) + EPS) * gain_buf[1].astype(F32)
             k_val = (t * cos_k[...] + pltpu.roll(t, half_head, 1) * sin_k[...]).astype(BF16)
-            v_val = raw[:, width // 2 + e * head:width // 2 + (e + 1) * head].T.astype(BF16)
+            v_val = v_raw[:, e * head:(e + 1) * head].T.astype(BF16)
             stage[idx, e, 0] = k_val
             stage[idx, e, 1] = v_val
 
@@ -199,6 +209,7 @@
         return carry
 
     lax.fori_loop(0, 4, project_kv, 0)
+    gain_t[...] = jnp.broadcast_to(gain_buf[0].astype(F32), (chip_rows, head)).T
     h_copy.wait_recv()
 
     def item_of(dirn, d):
@@ -210,21 +221,21 @@
     def goes_on(dirn, d):
         return arrives(dirn, d) & (chip < chips - 1) if dirn == 0 else arrives(dirn, d)
 
-    def ring_copy(dirn, j, d, whole):
-        item = item_of(dirn, d - 1)
-        sem = (d - 2) * local_heads + j
-        ref = kv.at[item, j] if whole else kv.at[item, j, dirn]
+    def ring_copy(dirn, j, d, item, part):
+        half = (dirn, 1 - dirn, None)[part]
+        sem = (d - 2) * local_heads + j + (2 * local_heads if part == REST else 0)
+        ref = kv.at[item, j] if half is None else kv.at[item, j, half]
         return pltpu.make_async_remote_copy(ref, ref, ring_ssem.at[dirn, sem], ring_rsem.at[dirn, sem], device_id=device(neighbour(dirn), core))
 
-    def landed(dirn, j, d, whole):
-        item = item_of(dirn, d)
-        sem = (d - 2) * local_heads + j
-        ref = kv.at[item, j] if whole else kv.at[item, j, dirn]
-        return pltpu.make_async_remote_copy(ref, ref, ring_ssem.at[dirn, sem], ring_rsem.at[dirn, sem], device_id=device(neighbour(dirn), core))
+    def outgoing(dirn, j, d, part):
+        return ring_copy(dirn, j, d, item_of(dirn, d - 1), part)
+
+    def landed(dirn, j, d, part):
+        return ring_copy(dirn, j, d, item_of(dirn, d), part)
 
     def forward_first(j):
         for dirn in range(2):
-            pl.when(goes_on(dirn, 1))(ring_copy(dirn, j, 2, True).start)
+            pl.when(goes_on(dirn, 1))(outgoing(dirn, j, 2, WHOLE).start)
 
     def poll_first(pair):
         for dirn in range(2):
@@ -238,20 +249,44 @@
         j = lookup(HEAD_TABLE, s)
         d = lookup(HOP_TABLE, s) + 1
         for dirn in range(2):
-            pl.when(arrives(dirn, d) & (d < far))(landed(dirn, j, d, True).wait_recv)
-            pl.when(arrives(dirn, d) & (d == far))(landed(dirn, j, d, False).wait_recv)
-            pl.when(goes_on(dirn, d) & (d + 1 < far))(ring_copy(dirn, j, d + 1, True).start)
-            pl.when(goes_on(dirn, d) & (d + 1 == far))(ring_copy(dirn, j, d + 1, False).start)
+            @pl.when(arrives(dirn, 2) & (d == 2))
+            def _():
+                landed(dirn, j, 2, WHOLE).wait_recv()
+
+            @pl.when(goes_on(dirn, 2) & (d == 2))
+            def _():
+                outgoing(dirn, j, 3, NEAR).start()
+                outgoing(dirn, j, 3, REST).start()
+
+            @pl.when(arrives(dirn, 3) & (d == 3))
+            def _():
+                landed(dirn, j, 3, NEAR).wait_recv()
+
+            @pl.when(goes_on(dirn, 3) & (d == 3))
+            def _():
+                outgoing(dirn, j, 4, NEAR).start()
+
+        for dirn in range(2):
+            @pl.when(arrives(dirn, 3) & (d == 3))
+            def _():
+                landed(dirn, j, 3, REST).wait_recv()
+
+            @pl.when(arrives(dirn, 4) & (d == 4))
+            def _():
+                landed(dirn, j, 4, NEAR).wait_recv()
 
     def drain(j, carry):
-        for d in range(1, far):
-            for dirn in range(2):
-                pl.when(goes_on(dirn, d))(ring_copy(dirn, j, d + 1, d + 1 < far).wait_send)
+        for dirn in range(2):
+            pl.when(goes_on(dirn, 1))(outgoing(dirn, j, 2, WHOLE).wait_send)
+            pl.when(goes_on(dirn, 2))(outgoing(dirn, j, 3, NEAR).wait_send)
+            pl.when(goes_on(dirn, 2))(outgoing(dirn, j, 3, REST).wait_send)
+            pl.when(goes_on(dirn, 3))(outgoing(dirn, j, 4, NEAR).wait_send)
         return carry
 
     def project_q(idx, carry):
         slot = (idx + 4) % 3
-        w_wait(slot)
+        for copy in q_copies(idx):
+            copy.wait()
         raw = dot(h_buf[...].reshape(chip_rows, dim), w_buf[slot])
 
         @pl.when(idx == 0)
@@ -332,30 +367,32 @@
     poll_first(1)
 
     def o_copy(k):
-        cols = pl.ds(stages[k][0] * width, (stages[k][1] - stages[k][0]) * width)
-        return pltpu.make_async_remote_copy(o_send.at[:, cols], o_all.at[core, :, cols], o_ssem.at[k], o_rsem.at[k], device_id={'sp': partner})
+        at, size = span_of(k, core)
+        target = pl.ds(pl.multiple_of(at, head), size)
+        return pltpu.make_async_remote_copy(o_send.at[:, pl.ds(stages[k][0] * width, size)], o_all.at[:, target], o_ssem.at[k], o_rsem.at[k],
+                                            device_id={'sp': partner})
 
     def close_head(j):
+        k = min(j // EARLY, 1) + max(0, j - EARLY)
+        at = span_of(k, core)[0] + (j - stages[k][0]) * width
         inv = 1.0 / jnp.sum(l_buf[j], axis=0, keepdims=True)
         for g in range(group):
             cols = slice(g * chip_rows, (g + 1) * chip_rows)
             o_val = (o_t[j, :, cols] * inv[:, cols]).T.astype(BF16)
-            out_cols = slice(j * width + g * head, j * width + (g + 1) * head)
-            o_all[core, :, out_cols] = jnp.where(core == 0, o_val[:rows], o_val[rows:])
-            o_send[:, out_cols] = jnp.where(core == 0, o_val[rows:], o_val[:rows])
+            o_all[:, pl.ds(pl.multiple_of(at + g * head, head), head)] = jnp.where(core == 0, o_val[:rows], o_val[rows:])
+            o_send[:, j * width + g * head:j * width + (g + 1) * head] = jnp.where(core == 0, o_val[rows:], o_val[:rows])
 
     def project_out(k, start, end):
-        first_head, last_head = stages[k]
         wo_wait(k)
         o_copy(k).wait_recv()
-        depth = slice(first_head * width, last_head * width)
+        at, size = span_of(k, 0)
+        depth = slice(at, at + CORES * size)
 
         def block(n, carry):
             for w in range(wide // width):
                 cols = pl.ds(pl.multiple_of(n * wide + w * width, width), width)
                 total = x_buf[:, cols].astype(F32) if start else acc[:, cols]
-                for c in range(CORES):
-                    total = total + dot(o_all[c, :, depth], wo_buf[c * mixed_dim + depth.start:c * mixed_dim + depth.stop, cols])
+                total = total + dot(o_all[:, depth], wo_buf[depth, cols])
                 if end:
                     out_ref[:, cols] = total.astype(BF16)
                 else:
@@ -456,7 +493,7 @@
                 pltpu.VMEM((local_heads, head, wide), F32),
                 pltpu.VMEM((local_heads, 8, wide), F32),
                 pltpu.VMEM((local_heads, 8, wide), F32),
-                pltpu.VMEM((CORES, rows, local_heads * width), BF16),
+                pltpu.VMEM((rows, w_o.shape[0]), BF16),
                 pltpu.VMEM((rows, local_heads * width), BF16),
                 pltpu.VMEM((rows, dim), F32),
                 pltpu.VMEM((dim // LANES, LANES), BF16),
@@ -465,10 +502,10 @@
                 pltpu.VMEM((head, chip_rows), F32),
                 pltpu.VMEM((rows, head), F32),
                 pltpu.VMEM((rows, head), F32),
-                dma((2,)), dma((4,)), dma((3,)), dma((3,)), dma, dma,
+                dma((2,)), dma((4,)), dma((3, 2)), dma((3,)), dma, dma,
                 dma((2,)), dma((2,)),
                 dma((2, 4)), dma((2, 2, CORES)),
-                dma((2, (chips // 2 - 1) * local_heads)), dma((2, (chips // 2 - 1) * local_heads)),
+                dma((2, 4 * local_heads)), dma((2, 4 * local_heads)),
                 dma((3,)), dma((3,)),
             ],
             compiler_params=pltpu.CompilerParams(collective_id=0, has_side_effects=True, vmem_limit_bytes=VMEM_LIMIT),

time: 52.7 us -> 53.3 us (1.011)
  the two profiles are of different devices: /device:TPU:182 before, /device:TPU:181 now
where the time goes in v5:
time: 53.3 us; the launch traced here: 53.2 us
  Pallas kernels  52.2 us (98%)
  local copies, waits for them, and re-layouts  0.97 us (2%)
    pallas_call x1, Pallas kernels, device_step(): pl.pallas_call(functools.partial(kernel, group_size), out_shape=pltpu.VME...  52.2 us

profile of v5, /device:TPU:181, one launch (start us, length us, event | category | flops | bytes accessed | tf_op | source)
XLA Modules:
  0.0 53.2 jit_solution(8469651954707257888)
XLA Ops:
  0.0 52.2 %shard_map.91 = bf16[128,4096]{1,0:T(8,128)(2,1)S(1)} custom-call(bf16[128,4096]{1,0:T(8,128)(2,1)} %x_hbm.1, bf16[4096,4096]{1,0:T(8,128)(2,1)} %wq.1, bf16[4096,1024]{1,0:T(8,128)(2,1)} %wk.1, bf16[4096,1024]{1,0:T(8,128)(2,1)} %wv.1, bf16[4096,4096]{1,0:T(8,128)(2,1)} %wo.1, bf16[32,128]{1,0:T(8,128)(2,1)} %bitcast.3, bf16[1,128]{1,0:T(2,128)(2,1)} %bitcast.4, ...), custom_call_target="tpu_custom_call" | custom-call | tf_op jit(solution)/shard_map/pallas_call | solution.py:480
  52.2 1.0 %copy.11 = bf16[128,4096]{1,0:T(8,128)(2,1)} copy(bf16[128,4096]{1,0:T(8,128)(2,1)S(1)} %shard_map.91) | data formatting | bytes 2097152

commit v6 on v5

--- a/solution.py
+++ b/solution.py
@@ -169,12 +169,9 @@
 
     def project_kv(idx, carry):
         slot = idx % 3
-        raws = []
-        for part, copy in enumerate(kv_copies(idx)):
+        for copy in kv_copies(idx):
             copy.wait()
-            cols = slice(part * (width // 2), (part + 1) * (width // 2))
-            raws.append(dot(h_buf[core, :, :dim // 2], w_buf[slot, :dim // 2, cols]) + dot(h_buf[core, :, dim // 2:], w_buf[slot, dim // 2:, cols]))
-        k_raw, v_raw = raws
+        raw = dot(h_buf[core], w_buf[slot])
 
         @pl.when(idx == 0)
         def _():
@@ -187,10 +184,10 @@
                 copy.start()
 
         for e in range(2):
-            t = k_raw[:, e * head:(e + 1) * head]
+            t = raw[:, e * head:(e + 1) * head]
             t = t * lax.rsqrt(jnp.mean(t * t, axis=-1, keepdims=True) + EPS) * gain_buf[1].astype(F32)
             k_val = (t * cos_k[...] + pltpu.roll(t, half_head, 1) * sin_k[...]).astype(BF16)
-            v_val = v_raw[:, e * head:(e + 1) * head].T.astype(BF16)
+            v_val = raw[:, width // 2 + e * head:width // 2 + (e + 1) * head].T.astype(BF16)
             stage[idx, e, 0] = k_val
             stage[idx, e, 1] = v_val
 
@@ -245,7 +242,7 @@
                     pltpu.make_async_remote_copy(stage.at[0], kv.at[item_of(dirn, 1), pl.ds(pair * 2, 2), k], first_ssem.at[0, 0],
                                                  first_rsem.at[dirn, pair, k], device_id={'sp': partner}).wait_recv()
 
-    def poll(s):
+    def poll_near(s):
         j = lookup(HEAD_TABLE, s)
         d = lookup(HOP_TABLE, s) + 1
         for dirn in range(2):
@@ -266,6 +263,9 @@
             def _():
                 outgoing(dirn, j, 4, NEAR).start()
 
+    def poll_rest(s):
+        j = lookup(HEAD_TABLE, s)
+        d = lookup(HOP_TABLE, s) + 1
         for dirn in range(2):
             @pl.when(arrives(dirn, 3) & (d == 3))
             def _():
@@ -382,15 +382,16 @@
             o_all[:, pl.ds(pl.multiple_of(at + g * head, head), head)] = jnp.where(core == 0, o_val[:rows], o_val[rows:])
             o_send[:, j * width + g * head:j * width + (g + 1) * head] = jnp.where(core == 0, o_val[rows:], o_val[:rows])
 
-    def project_out(k, start, end):
-        wo_wait(k)
-        o_copy(k).wait_recv()
+    def project_out(k, start, end, half=None):
+        if half in (None, 0):
+            wo_wait(k)
+            o_copy(k).wait_recv()
         at, size = span_of(k, 0)
         depth = slice(at, at + CORES * size)
 
         def block(n, carry):
             for w in range(wide // width):
-                cols = pl.ds(pl.multiple_of(n * wide + w * width, width), width)
+                cols = pl.ds(n * wide + w * width, width) if isinstance(n, int) else pl.ds(pl.multiple_of(n * wide + w * width, width), width)
                 total = x_buf[:, cols].astype(F32) if start else acc[:, cols]
                 total = total + dot(o_all[:, depth], wo_buf[depth, cols])
                 if end:
@@ -400,17 +401,15 @@
             return carry
 
         wide = dim // 2
-        lax.fori_loop(0, dim // wide, block, 0)
+        if half is None:
+            lax.fori_loop(0, dim // wide, block, 0)
+        else:
+            block(half, 0)
 
     def ring_step(s, carry):
         @pl.when(s >= local_heads)
         def _():
-            poll(s)
-
-        for at, j in DEFERRED:
-            @pl.when(s == at)
-            def _():
-                forward_first(j)
+            poll_rest(s)
 
         j = lookup(HEAD_TABLE, s)
         d = lookup(HOP_TABLE, s) + 1
@@ -424,15 +423,25 @@
         def _():
             attend((item_of(0, d),), j, ahead=group)
 
+        @pl.when((s + 1 >= local_heads) & (s + 1 < SLOTS))
+        def _():
+            poll_near(s + 1)
+
+        for at, late in DEFERRED:
+            @pl.when(s + 1 == at)
+            def _():
+                forward_first(late)
+
         @pl.when(s == EARLY_CLOSE)
         def _():
             for early in range(EARLY):
                 close_head(early)
             o_copy(0).start()
 
-        @pl.when(s == EARLY_OUT)
-        def _():
-            project_out(0, True, False)
+        for half in range(2):
+            @pl.when(s == EARLY_OUT + half)
+            def _():
+                project_out(0, True, False, half)
 
         @pl.when(s == THIRD_CLOSE)
         def _():

time: 53.3 us -> 52.4 us (0.983)
  the two profiles are of different devices: /device:TPU:181 before, /device:TPU:221 now
where the time goes in v6:
time: 52.4 us; the launch traced here: 52.2 us
  Pallas kernels  51.3 us (98%)
  local copies, waits for them, and re-layouts  0.97 us (2%)
    pallas_call x1, Pallas kernels, device_step(): pl.pallas_call(functools.partial(kernel, group_size), out_shape=pltpu.VME...  51.3 us

profile of v6, /device:TPU:221, one launch (start us, length us, event | category | flops | bytes accessed | tf_op | source)
XLA Modules:
  0.0 52.2 jit_solution(16803082131034815536)
XLA Ops:
  0.0 51.3 %shard_map.91 = bf16[128,4096]{1,0:T(8,128)(2,1)S(1)} custom-call(bf16[128,4096]{1,0:T(8,128)(2,1)} %x_hbm.1, bf16[4096,4096]{1,0:T(8,128)(2,1)} %wq.1, bf16[4096,1024]{1,0:T(8,128)(2,1)} %wk.1, bf16[4096,1024]{1,0:T(8,128)(2,1)} %wv.1, bf16[4096,4096]{1,0:T(8,128)(2,1)} %wo.1, bf16[32,128]{1,0:T(8,128)(2,1)} %bitcast.3, bf16[1,128]{1,0:T(2,128)(2,1)} %bitcast.4, ...), custom_call_target="tpu_custom_call" | custom-call | tf_op jit(solution)/shard_map/pallas_call | solution.py:489
  51.3 1.0 %copy.11 = bf16[128,4096]{1,0:T(8,128)(2,1)} copy(bf16[128,4096]{1,0:T(8,128)(2,1)S(1)} %shard_map.91) | data formatting | bytes 2097152

commit v7 on v6

--- a/solution.py
+++ b/solution.py
@@ -89,6 +89,14 @@
         return (pltpu.make_async_copy(wk.at[:, cols], w_buf.at[slot, :, pl.ds(0, width // 2)], w_sem.at[slot, 0]),
                 pltpu.make_async_copy(wv.at[:, cols], w_buf.at[slot, :, pl.ds(width // 2, width // 2)], w_sem.at[slot, 1]))
 
+    def lead_copies(e):
+        cols = pl.ds(e * head, head)
+        return tuple(pltpu.make_async_copy(w.at[:, cols], w_buf.at[0, :, pl.ds((2 * e + part) * head, head)], w_sem.at[0, e])
+                     for part, w in enumerate((wk, wv)))
+
+    def lead_wait(e):
+        pltpu.make_async_copy(wk.at[:, pl.ds(0, 2 * head)], w_buf.at[0, :, pl.ds(2 * e * head, 2 * head)], w_sem.at[0, e]).wait()
+
     def q_copies(idx):
         cols = pl.ds(pl.multiple_of((core * local_heads + idx) * width, width), width)
         slot = (idx + 4) % 3
@@ -120,7 +128,8 @@
         x_copy(r).start()
     for copy in small[1:]:
         copy.start()
-    kv_copies(0)[0].start()
+    for copy in lead_copies(0):
+        copy.start()
 
     barrier = pltpu.get_barrier_semaphore()
     pl.semaphore_signal(barrier, inc=1, device_id={'sp': partner})
@@ -132,11 +141,11 @@
     for r in range(x_parts):
         x_copy(r).wait()
         if r == 0:
-            kv_copies(0)[1].start()
+            for copy in lead_copies(1):
+                copy.start()
         if r == x_parts - 1:
-            for idx in range(1, 3):
-                for copy in kv_copies(idx):
-                    copy.start()
+            for copy in kv_copies(1):
+                copy.start()
         step_rows = 16
         for t in range(part_rows // step_rows):
             sl = slice(r * part_rows + t * step_rows, r * part_rows + (t + 1) * step_rows)
@@ -157,55 +166,55 @@
     pl.semaphore_wait(barrier, 1 + 2 * CORES)
     h_copy = pltpu.make_async_remote_copy(h_buf.at[core], h_buf.at[core], h_ssem, h_rsem, device_id={'sp': partner})
 
-    def first_copies(idx):
+    def first_copies(idx, e=None):
         owner = idx % 2
         pair = idx // 2
-        src = stage.at[idx]
-        dst = kv.at[chip, pl.ds(pair * 2, 2), core]
+        src = stage.at[idx] if e is None else stage.at[idx, e]
+        dst = kv.at[chip, pl.ds(pair * 2, 2), core] if e is None else kv.at[chip, e, core]
         up = pltpu.make_async_remote_copy(src, dst, first_ssem.at[0, idx], first_rsem.at[0, pair, core], device_id=device(neighbour(0), owner))
         down = pltpu.make_async_remote_copy(src, dst, first_ssem.at[1, idx], first_rsem.at[1, pair, core], device_id=device(neighbour(1), owner))
         across = pltpu.make_async_remote_copy(src, dst, d2d_ssem.at[pair], d2d_rsem.at[pair], device_id={'sp': partner})
         return ((up, chip < chips - 1), (down, chip < far), (across, owner != core))
+
+    def keep_kv(idx, e, k_raw, v_raw):
+        t = k_raw * lax.rsqrt(jnp.mean(k_raw * k_raw, axis=-1, keepdims=True) + EPS) * gain_buf[1].astype(F32)
+        k_val = (t * cos_k[...] + pltpu.roll(t, half_head, 1) * sin_k[...]).astype(BF16)
+        v_val = v_raw.T.astype(BF16)
+        stage[idx, e, 0] = k_val
+        stage[idx, e, 1] = v_val
+
+        @pl.when(idx % 2 == core)
+        def _():
+            kv[chip, (idx // 2) * 2 + e, core, 0] = k_val
+            kv[chip, (idx // 2) * 2 + e, core, 1] = v_val
+
+    for e in range(2):
+        lead_wait(e)
+        raw = dot(h_buf[core], w_buf[0, :, 2 * e * head:2 * (e + 1) * head])
+        if e == 0:
+            for copy in kv_copies(2):
+                copy.start()
+        keep_kv(0, e, raw[:, :head], raw[:, head:])
+        for copy, cond in first_copies(0, e):
+            pl.when(cond)(copy.start)
+    for copy in kv_copies(3):
+        copy.start()
+    h_copy.start()
 
     def project_kv(idx, carry):
         slot = idx % 3
         for copy in kv_copies(idx):
             copy.wait()
         raw = dot(h_buf[core], w_buf[slot])
-
-        @pl.when(idx == 0)
-        def _():
-            for copy in kv_copies(3):
-                copy.start()
-
-        @pl.when(idx > 0)
-        def _():
-            for copy in q_copies(idx - 1):
-                copy.start()
-
+        for copy in q_copies(idx - 1):
+            copy.start()
         for e in range(2):
-            t = raw[:, e * head:(e + 1) * head]
-            t = t * lax.rsqrt(jnp.mean(t * t, axis=-1, keepdims=True) + EPS) * gain_buf[1].astype(F32)
-            k_val = (t * cos_k[...] + pltpu.roll(t, half_head, 1) * sin_k[...]).astype(BF16)
-            v_val = raw[:, width // 2 + e * head:width // 2 + (e + 1) * head].T.astype(BF16)
-            stage[idx, e, 0] = k_val
-            stage[idx, e, 1] = v_val
-
-            @pl.when(idx % 2 == core)
-            def _():
-                kv[chip, (idx // 2) * 2 + e, core, 0] = k_val
-                kv[chip, (idx // 2) * 2 + e, core, 1] = v_val
-
+            keep_kv(idx, e, raw[:, e * head:(e + 1) * head], raw[:, width // 2 + e * head:width // 2 + (e + 1) * head])
         for copy, cond in first_copies(idx):
             pl.when(cond)(copy.start)
-
-        @pl.when(idx == 0)
-        def _():
-            h_copy.start()
-
         return carry
 
-    lax.fori_loop(0, 4, project_kv, 0)
+    lax.fori_loop(1, 4, project_kv, 0)
     gain_t[...] = jnp.broadcast_to(gain_buf[0].astype(F32), (chip_rows, head)).T
     h_copy.wait_recv()
 

time: 52.4 us -> 52.1 us (level)
  the two profiles are of different devices: /device:TPU:221 before, /device:TPU:213 now
where the time goes in v7:
time: 52.1 us; the launch traced here: 52 us
  Pallas kernels  51 us (98%)
  local copies, waits for them, and re-layouts  0.97 us (2%)
    pallas_call x1, Pallas kernels, device_step(): pl.pallas_call(functools.partial(kernel, group_size), out_shape=pltpu.VME...  51 us

profile of v7, /device:TPU:213, one launch (start us, length us, event | category | flops | bytes accessed | tf_op | source)
XLA Modules:
  0.0 52.0 jit_solution(8148987481904166566)
XLA Ops:
  0.0 51.0 %shard_map.91 = bf16[128,4096]{1,0:T(8,128)(2,1)S(1)} custom-call(bf16[128,4096]{1,0:T(8,128)(2,1)} %x_hbm.1, bf16[4096,4096]{1,0:T(8,128)(2,1)} %wq.1, bf16[4096,1024]{1,0:T(8,128)(2,1)} %wk.1, bf16[4096,1024]{1,0:T(8,128)(2,1)} %wv.1, bf16[4096,4096]{1,0:T(8,128)(2,1)} %wo.1, bf16[32,128]{1,0:T(8,128)(2,1)} %bitcast.3, bf16[1,128]{1,0:T(2,128)(2,1)} %bitcast.4, ...), custom_call_target="tpu_custom_call" | custom-call | tf_op jit(solution)/shard_map/pallas_call | solution.py:498
  51.0 1.0 %copy.11 = bf16[128,4096]{1,0:T(8,128)(2,1)} copy(bf16[128,4096]{1,0:T(8,128)(2,1)S(1)} %shard_map.91) | data formatting | bytes 2097152

commit v8 on v7

--- a/solution.py
+++ b/solution.py
@@ -24,6 +24,7 @@
 ORDER = ((0, 1), (1, 1), (2, 1), (3, 1), (0, 2), (1, 2), (0, 3), (1, 3), (2, 2), (0, 4), (1, 4), (3, 2), (2, 3), (3, 3), (2, 4), (3, 4))
 SLOTS = len(ORDER)
 EARLY = 2
+FIRST_POLL = 1
 EARLY_CLOSE = 10
 EARLY_OUT = 11
 THIRD_CLOSE = 14
@@ -171,8 +172,8 @@
         pair = idx // 2
         src = stage.at[idx] if e is None else stage.at[idx, e]
         dst = kv.at[chip, pl.ds(pair * 2, 2), core] if e is None else kv.at[chip, e, core]
-        up = pltpu.make_async_remote_copy(src, dst, first_ssem.at[0, idx], first_rsem.at[0, pair, core], device_id=device(neighbour(0), owner))
-        down = pltpu.make_async_remote_copy(src, dst, first_ssem.at[1, idx], first_rsem.at[1, pair, core], device_id=device(neighbour(1), owner))
+        up = pltpu.make_async_remote_copy(src, dst, first_ssem.at[0, idx], first_rsem.at[0, pair], device_id=device(neighbour(0), owner))
+        down = pltpu.make_async_remote_copy(src, dst, first_ssem.at[1, idx], first_rsem.at[1, pair], device_id=device(neighbour(1), owner))
         across = pltpu.make_async_remote_copy(src, dst, d2d_ssem.at[pair], d2d_rsem.at[pair], device_id={'sp': partner})
         return ((up, chip < chips - 1), (down, chip < far), (across, owner != core))
 
@@ -231,7 +232,7 @@
         half = (dirn, 1 - dirn, None)[part]
         sem = (d - 2) * local_heads + j + (2 * local_heads if part == REST else 0)
         ref = kv.at[item, j] if half is None else kv.at[item, j, half]
-        return pltpu.make_async_remote_copy(ref, ref, ring_ssem.at[dirn, sem], ring_rsem.at[dirn, sem], device_id=device(neighbour(dirn), core))
+        return pltpu.make_async_remote_copy(ref, ref, ring_ssem.at[dirn, j + (local_heads if part == REST else 0)], ring_rsem.at[dirn, sem], device_id=device(neighbour(dirn), core))
 
     def outgoing(dirn, j, d, part):
         return ring_copy(dirn, j, d, item_of(dirn, d - 1), part)
@@ -247,9 +248,8 @@
         for dirn in range(2):
             @pl.when(arrives(dirn, 1))
             def _():
-                for k in range(CORES):
-                    pltpu.make_async_remote_copy(stage.at[0], kv.at[item_of(dirn, 1), pl.ds(pair * 2, 2), k], first_ssem.at[0, 0],
-                                                 first_rsem.at[dirn, pair, k], device_id={'sp': partner}).wait_recv()
+                both = kv.at[item_of(dirn, 1), pl.ds(pair * 2, 2)]
+                pltpu.make_async_remote_copy(both, both, first_ssem.at[0, 0], first_rsem.at[dirn, pair], device_id={'sp': partner}).wait_recv()
 
     def poll_near(s):
         j = lookup(HEAD_TABLE, s)
@@ -261,6 +261,7 @@
 
             @pl.when(goes_on(dirn, 2) & (d == 2))
             def _():
+                pl.when(goes_on(dirn, 1))(outgoing(dirn, j, 2, WHOLE).wait_send)
                 outgoing(dirn, j, 3, NEAR).start()
                 outgoing(dirn, j, 3, REST).start()
 
@@ -270,6 +271,7 @@
 
             @pl.when(goes_on(dirn, 3) & (d == 3))
             def _():
+                pl.when(goes_on(dirn, 2))(outgoing(dirn, j, 3, NEAR).wait_send)
                 outgoing(dirn, j, 4, NEAR).start()
 
     def poll_rest(s):
@@ -286,10 +288,11 @@
 
     def drain(j, carry):
         for dirn in range(2):
-            pl.when(goes_on(dirn, 1))(outgoing(dirn, j, 2, WHOLE).wait_send)
-            pl.when(goes_on(dirn, 2))(outgoing(dirn, j, 3, NEAR).wait_send)
-            pl.when(goes_on(dirn, 2))(outgoing(dirn, j, 3, REST).wait_send)
-            pl.when(goes_on(dirn, 3))(outgoing(dirn, j, 4, NEAR).wait_send)
+            on = [goes_on(dirn, d) for d in range(4)]
+            pl.when(on[1] & jnp.logical_not(on[2]))(outgoing(dirn, j, 2, WHOLE).wait_send)
+            pl.when(on[2] & jnp.logical_not(on[3]))(outgoing(dirn, j, 3, NEAR).wait_send)
+            pl.when(on[2])(outgoing(dirn, j, 3, REST).wait_send)
+            pl.when(on[3])(outgoing(dirn, j, 4, NEAR).wait_send)
         return carry
 
     def project_q(idx, carry):
@@ -398,22 +401,19 @@
         at, size = span_of(k, 0)
         depth = slice(at, at + CORES * size)
 
-        def block(n, carry):
+        def block(n):
             for w in range(wide // width):
-                cols = pl.ds(n * wide + w * width, width) if isinstance(n, int) else pl.ds(pl.multiple_of(n * wide + w * width, width), width)
+                cols = pl.ds(n * wide + w * width, width)
                 total = x_buf[:, cols].astype(F32) if start else acc[:, cols]
                 total = total + dot(o_all[:, depth], wo_buf[depth, cols])
                 if end:
                     out_ref[:, cols] = total.astype(BF16)
                 else:
                     acc[:, cols] = total
-            return carry
 
         wide = dim // 2
-        if half is None:
-            lax.fori_loop(0, dim // wide, block, 0)
-        else:
-            block(half, 0)
+        for n in range(dim // wide) if half is None else (half,):
+            block(n)
 
     def ring_step(s, carry):
         @pl.when(s >= local_heads)
@@ -432,20 +432,20 @@
         def _():
             attend((item_of(0, d),), j, ahead=group)
 
-        @pl.when((s + 1 >= local_heads) & (s + 1 < SLOTS))
-        def _():
-            poll_near(s + 1)
-
-        for at, late in DEFERRED:
-            @pl.when(s + 1 == at)
-            def _():
-                forward_first(late)
-
         @pl.when(s == EARLY_CLOSE)
         def _():
             for early in range(EARLY):
                 close_head(early)
             o_copy(0).start()
+
+        @pl.when((s == FIRST_POLL) | ((s + 1 > local_heads) & (s + 1 < SLOTS)))
+        def _():
+            poll_near(jnp.where(s == FIRST_POLL, local_heads, s + 1))
+
+        for at, late in DEFERRED:
+            @pl.when(s + 1 == at)
+            def _():
+                forward_first(late)
 
         for half in range(2):
             @pl.when(s == EARLY_OUT + half)
@@ -522,8 +522,8 @@
                 pltpu.VMEM((rows, head), F32),
                 dma((2,)), dma((4,)), dma((3, 2)), dma((3,)), dma, dma,
                 dma((2,)), dma((2,)),
-                dma((2, 4)), dma((2, 2, CORES)),
-                dma((2, 4 * local_heads)), dma((2, 4 * local_heads)),
+                dma((2, 4)), dma((2, 2)),
+                dma((2, 2 * local_heads)), dma((2, 4 * local_heads)),
                 dma((3,)), dma((3,)),
             ],
             compiler_params=pltpu.CompilerParams(collective_id=0, has_side_effects=True, vmem_limit_bytes=VMEM_LIMIT),

time: 52.1 us -> 52.9 us (1.015)
  the two profiles are of different devices: /device:TPU:213 before, /device:TPU:21 now
where the time goes in v8:
time: 52.9 us; the launch traced here: 52.8 us
  Pallas kernels  51.8 us (98%)
  local copies, waits for them, and re-layouts  0.97 us (2%)
    pallas_call x1, Pallas kernels, device_step(): pl.pallas_call(functools.partial(kernel, group_size), out_shape=pltpu.VME...  51.8 us

profile of v8, /device:TPU:21, one launch (start us, length us, event | category | flops | bytes accessed | tf_op | source)
XLA Modules:
  0.0 52.8 jit_solution(10299546956937631035)
XLA Ops:
  0.0 51.8 %shard_map.91 = bf16[128,4096]{1,0:T(8,128)(2,1)S(1)} custom-call(bf16[128,4096]{1,0:T(8,128)(2,1)} %x_hbm.1, bf16[4096,4096]{1,0:T(8,128)(2,1)} %wq.1, bf16[4096,1024]{1,0:T(8,128)(2,1)} %wk.1, bf16[4096,1024]{1,0:T(8,128)(2,1)} %wv.1, bf16[4096,4096]{1,0:T(8,128)(2,1)} %wo.1, bf16[32,128]{1,0:T(8,128)(2,1)} %bitcast.3, bf16[1,128]{1,0:T(2,128)(2,1)} %bitcast.4, ...), custom_call_target="tpu_custom_call" | custom-call | tf_op jit(solution)/shard_map/pallas_call | solution.py:498
  51.8 1.0 %copy.11 = bf16[128,4096]{1,0:T(8,128)(2,1)} copy(bf16[128,4096]{1,0:T(8,128)(2,1)S(1)} %shard_map.91) | data formatting | bytes 2097152

commit v9 on v8

--- a/solution.py
+++ b/solution.py
@@ -25,6 +25,9 @@
 SLOTS = len(ORDER)
 EARLY = 2
 FIRST_POLL = 1
+LOW_CHIPS = 2
+LOW_CLOSE = 7
+LOW_OUT = 9
 EARLY_CLOSE = 10
 EARLY_OUT = 11
 THIRD_CLOSE = 14
@@ -432,12 +435,24 @@
         def _():
             attend((item_of(0, d),), j, ahead=group)
 
-        @pl.when(s == EARLY_CLOSE)
+        low = chip < LOW_CHIPS
+
+        @pl.when(s == jnp.where(low, LOW_CLOSE, EARLY_CLOSE))
         def _():
             for early in range(EARLY):
                 close_head(early)
             o_copy(0).start()
 
+        @pl.when(s == jnp.where(low, LOW_CLOSE, THIRD_CLOSE))
+        def _():
+            close_head(EARLY)
+            o_copy(1).start()
+
+        @pl.when(s == jnp.where(low, LOW_CLOSE, SLOTS - 1))
+        def _():
+            close_head(local_heads - 1)
+            o_copy(2).start()
+
         @pl.when((s == FIRST_POLL) | ((s + 1 > local_heads) & (s + 1 < SLOTS)))
         def _():
             poll_near(jnp.where(s == FIRST_POLL, local_heads, s + 1))
@@ -448,22 +463,21 @@
                 forward_first(late)
 
         for half in range(2):
-            @pl.when(s == EARLY_OUT + half)
+            @pl.when(s == jnp.where(low, LOW_OUT, EARLY_OUT + half))
             def _():
                 project_out(0, True, False, half)
 
-        @pl.when(s == THIRD_CLOSE)
-        def _():
-            close_head(EARLY)
-            o_copy(1).start()
+        @pl.when(s == jnp.where(low, LOW_OUT, SLOTS - 1))
+        def _():
+            project_out(1, False, False)
+
+        @pl.when(s == jnp.where(low, LOW_OUT, SLOTS - 1))
+        def _():
+            project_out(2, False, True)
 
         return carry
 
     lax.fori_loop(0, SLOTS, ring_step, 0)
-    close_head(local_heads - 1)
-    o_copy(2).start()
-    project_out(1, False, False)
-    project_out(2, False, True)
 
     h_copy.wait_send()
     for k in range(len(stages)):

time: 52.9 us -> 50.4 us (0.953)
  Pallas kernels: 51.8 us -> 49.1 us
    pallas_call x1, Pallas kernels: 51.8 us -> 49.1 us  [device_step(): pl.pallas_call(functools.partial(kernel, group_size), out_shape=pltpu.VME...]
where the time goes in v9:
time: 50.4 us; the launch traced here: 50.1 us
  Pallas kernels  49.1 us (97%)
  local copies, waits for them, and re-layouts  0.97 us (2%)
    pallas_call x1, Pallas kernels, device_step(): pl.pallas_call(functools.partial(kernel, group_size), out_shape=pltpu.VME...  49.1 us

profile of v9, /device:TPU:21, one launch (start us, length us, event | category | flops | bytes accessed | tf_op | source)
XLA Modules:
  0.0 50.1 jit_solution(8276438475491247979)
XLA Ops:
  0.0 49.1 %shard_map.91 = bf16[128,4096]{1,0:T(8,128)(2,1)S(1)} custom-call(bf16[128,4096]{1,0:T(8,128)(2,1)} %x_hbm.1, bf16[4096,4096]{1,0:T(8,128)(2,1)} %wq.1, bf16[4096,1024]{1,0:T(8,128)(2,1)} %wk.1, bf16[4096,1024]{1,0:T(8,128)(2,1)} %wv.1, bf16[4096,4096]{1,0:T(8,128)(2,1)} %wo.1, bf16[32,128]{1,0:T(8,128)(2,1)} %bitcast.3, bf16[1,128]{1,0:T(2,128)(2,1)} %bitcast.4, ...), custom_call_target="tpu_custom_call" | custom-call | tf_op jit(solution)/shard_map/pallas_call | solution.py:512
  49.1 1.0 %copy.11 = bf16[128,4096]{1,0:T(8,128)(2,1)} copy(bf16[128,4096]{1,0:T(8,128)(2,1)S(1)} %shard_map.91) | data formatting | bytes 2097152

commit v10 on v9

--- a/solution.py
+++ b/solution.py
@@ -143,8 +143,16 @@
 
     small[0].wait()
     for r in range(x_parts):
+        if r == x_parts - 1:
+            for copy in small[1:]:
+                copy.wait()
+            own_cols = pl.ds(pl.multiple_of(core * rows, rows), rows)
+            cos_own = angle_t[0, :, own_cols].T
+            sin_own = angle_t[1, :, own_cols].T
+            cos_k[...] = jnp.concatenate([cos_own, cos_own], axis=1)
+            sin_k[...] = jnp.concatenate([-sin_own, sin_own], axis=1)
         x_copy(r).wait()
-        if r == 0:
+        if r == 1:
             for copy in lead_copies(1):
                 copy.start()
         if r == x_parts - 1:
@@ -159,14 +167,6 @@
                 cols = slice(b * lanes, (b + 1) * lanes)
                 h_buf[core, sl, cols] = (xf[:, cols] * scale * ln_buf[b:b + 1, :].astype(F32)).astype(BF16)
 
-    for copy in small[1:]:
-        copy.wait()
-    own_cols = pl.ds(pl.multiple_of(core * rows, rows), rows)
-    cos_own = angle_t[0, :, own_cols].T
-    sin_own = angle_t[1, :, own_cols].T
-    cos_k[...] = jnp.concatenate([cos_own, cos_own], axis=1)
-    sin_k[...] = jnp.concatenate([-sin_own, sin_own], axis=1)
-
     pl.semaphore_wait(barrier, 1 + 2 * CORES)
     h_copy = pltpu.make_async_remote_copy(h_buf.at[core], h_buf.at[core], h_ssem, h_rsem, device_id={'sp': partner})
 
@@ -194,7 +194,9 @@
 
     for e in range(2):
         lead_wait(e)
-        raw = dot(h_buf[core], w_buf[0, :, 2 * e * head:2 * (e + 1) * head])
+        both = slice(2 * e * head, 2 * (e + 1) * head)
+        o_t[e, :rows, :2 * head] = dot(h_buf[core, :, :dim // 2], w_buf[0, :dim // 2, both])
+        raw = dot(h_buf[core, :, dim // 2:], w_buf[0, dim // 2:, both]) + o_t[e, :rows, :2 * head]
         if e == 0:
             for copy in kv_copies(2):
                 copy.start()
@@ -235,7 +237,7 @@
         half = (dirn, 1 - dirn, None)[part]
         sem = (d - 2) * local_heads + j + (2 * local_heads if part == REST else 0)
         ref = kv.at[item, j] if half is None else kv.at[item, j, half]
-        return pltpu.make_async_remote_copy(ref, ref, ring_ssem.at[dirn, j + (local_heads if part == REST else 0)], ring_rsem.at[dirn, sem], device_id=device(neighbour(dirn), core))
+        return pltpu.make_async_remote_copy(ref, ref, ring_ssem.at[dirn, local_heads if part == REST else j], ring_rsem.at[dirn, sem], device_id=device(neighbour(dirn), core))
 
     def outgoing(dirn, j, d, part):
         return ring_copy(dirn, j, d, item_of(dirn, d - 1), part)
@@ -294,7 +296,6 @@
             on = [goes_on(dirn, d) for d in range(4)]
             pl.when(on[1] & jnp.logical_not(on[2]))(outgoing(dirn, j, 2, WHOLE).wait_send)
             pl.when(on[2] & jnp.logical_not(on[3]))(outgoing(dirn, j, 3, NEAR).wait_send)
-            pl.when(on[2])(outgoing(dirn, j, 3, REST).wait_send)
             pl.when(on[3])(outgoing(dirn, j, 4, NEAR).wait_send)
         return carry
 
@@ -384,7 +385,7 @@
     def o_copy(k):
         at, size = span_of(k, core)
         target = pl.ds(pl.multiple_of(at, head), size)
-        return pltpu.make_async_remote_copy(o_send.at[:, pl.ds(stages[k][0] * width, size)], o_all.at[:, target], o_ssem.at[k], o_rsem.at[k],
+        return pltpu.make_async_remote_copy(o_send.at[:, pl.ds(stages[k][0] * width, size)], o_all.at[:, target], o_ssem, o_rsem.at[k],
                                             device_id={'sp': partner})
 
     def close_head(j):
@@ -480,8 +481,7 @@
     lax.fori_loop(0, SLOTS, ring_step, 0)
 
     h_copy.wait_send()
-    for k in range(len(stages)):
-        o_copy(k).wait_send()
+    pltpu.make_async_remote_copy(o_send, o_all.at[:, pl.ds(0, mixed_dim)], o_ssem, o_rsem.at[0], device_id={'sp': partner}).wait_send()
 
     def drain_first(idx, carry):
         for copy, cond in first_copies(idx):
@@ -490,6 +490,11 @@
 
     lax.fori_loop(0, 4, drain_first, 0)
     lax.fori_loop(0, local_heads, drain, 0)
+    for dirn in range(2):
+        @pl.when(goes_on(dirn, 2))
+        def _():
+            rest = kv.at[item_of(dirn, 2), :, 1 - dirn]
+            pltpu.make_async_remote_copy(rest, rest, ring_ssem.at[dirn, local_heads], ring_rsem.at[dirn, 0], device_id=device(neighbour(dirn), core)).wait_send()
 
 
 def solution(mesh):
@@ -534,11 +539,11 @@
                 pltpu.VMEM((head, chip_rows), F32),
                 pltpu.VMEM((rows, head), F32),
                 pltpu.VMEM((rows, head), F32),
-                dma((2,)), dma((4,)), dma((3, 2)), dma((3,)), dma, dma,
+                dma((4,)), dma((4,)), dma((3, 2)), dma((3,)), dma, dma,
                 dma((2,)), dma((2,)),
                 dma((2, 4)), dma((2, 2)),
-                dma((2, 2 * local_heads)), dma((2, 4 * local_heads)),
-                dma((3,)), dma((3,)),
+                dma((2, local_heads + 1)), dma((2, 4 * local_heads)),
+                dma, dma((3,)),
             ],
             compiler_params=pltpu.CompilerParams(collective_id=0, has_side_effects=True, vmem_limit_bytes=VMEM_LIMIT),
         )(hidden, w_q, w_k, w_v, w_o, ln_gain.reshape(-1, LANES), q_gain[None, :], k_gain[None, :], angle_all)

time: 50.4 us -> 50.3 us (level)
  no operation moved by 1% of the time
where the time goes in v10:
time: 50.3 us; the launch traced here: 49.9 us
  Pallas kernels  48.9 us (97%)
  local copies, waits for them, and re-layouts  0.97 us (2%)
    pallas_call x1, Pallas kernels, device_step(): pl.pallas_call(functools.partial(kernel, group_size), out_shape=pltpu.VME...  48.9 us

profile of v10, /device:TPU:21, one launch (start us, length us, event | category | flops | bytes accessed | tf_op | source)
XLA Modules:
  0.0 49.9 jit_solution(12440629346877356622)
XLA Ops:
  0.0 48.9 %shard_map.91 = bf16[128,4096]{1,0:T(8,128)(2,1)S(1)} custom-call(bf16[128,4096]{1,0:T(8,128)(2,1)} %x_hbm.1, bf16[4096,4096]{1,0:T(8,128)(2,1)} %wq.1, bf16[4096,1024]{1,0:T(8,128)(2,1)} %wk.1, bf16[4096,1024]{1,0:T(8,128)(2,1)} %wv.1, bf16[4096,4096]{1,0:T(8,128)(2,1)} %wo.1, bf16[32,128]{1,0:T(8,128)(2,1)} %bitcast.3, bf16[1,128]{1,0:T(2,128)(2,1)} %bitcast.4, ...), custom_call_target="tpu_custom_call" | custom-call | tf_op jit(solution)/shard_map/pallas_call | solution.py:517
  48.9 1.0 %copy.11 = bf16[128,4096]{1,0:T(8,128)(2,1)} copy(bf16[128,4096]{1,0:T(8,128)(2,1)S(1)} %shard_map.91) | data formatting | bytes 2097152

commit v11 on v10

--- a/solution.py
+++ b/solution.py
@@ -398,26 +398,27 @@
             o_all[:, pl.ds(pl.multiple_of(at + g * head, head), head)] = jnp.where(core == 0, o_val[:rows], o_val[rows:])
             o_send[:, j * width + g * head:j * width + (g + 1) * head] = jnp.where(core == 0, o_val[rows:], o_val[:rows])
 
-    def project_out(k, start, end, half=None):
-        if half in (None, 0):
-            wo_wait(k)
-            o_copy(k).wait_recv()
-        at, size = span_of(k, 0)
+    def project_early(half):
+        if half == 0:
+            wo_wait(0)
+            o_copy(0).wait_recv()
+        at, size = span_of(0, 0)
         depth = slice(at, at + CORES * size)
-
-        def block(n):
-            for w in range(wide // width):
-                cols = pl.ds(n * wide + w * width, width)
-                total = x_buf[:, cols].astype(F32) if start else acc[:, cols]
-                total = total + dot(o_all[:, depth], wo_buf[depth, cols])
-                if end:
-                    out_ref[:, cols] = total.astype(BF16)
-                else:
-                    acc[:, cols] = total
-
-        wide = dim // 2
-        for n in range(dim // wide) if half is None else (half,):
-            block(n)
+        for n in range(dim // 2 // width):
+            cols = pl.ds(half * (dim // 2) + n * width, width)
+            acc[:, cols] = x_buf[:, cols].astype(F32) + dot(o_all[:, depth], wo_buf[depth, cols])
+
+    def project_late(parts, end):
+        for n in range(dim // width):
+            cols = pl.ds(n * width, width)
+            total = acc[:, cols]
+            for k, c in parts:
+                at, size = span_of(k, c)
+                total = total + dot(o_all[:, pl.ds(pl.multiple_of(at, size), size)], wo_buf[pl.ds(pl.multiple_of(at, size), size), cols])
+            if end:
+                out_ref[:, cols] = total.astype(BF16)
+            else:
+                acc[:, cols] = total
 
     def ring_step(s, carry):
         @pl.when(s >= local_heads)
@@ -466,15 +467,17 @@
         for half in range(2):
             @pl.when(s == jnp.where(low, LOW_OUT, EARLY_OUT + half))
             def _():
-                project_out(0, True, False, half)
+                project_early(half)
 
         @pl.when(s == jnp.where(low, LOW_OUT, SLOTS - 1))
         def _():
-            project_out(1, False, False)
-
-        @pl.when(s == jnp.where(low, LOW_OUT, SLOTS - 1))
-        def _():
-            project_out(2, False, True)
+            for k in (1, 2):
+                wo_wait(k)
+            project_late(((1, core), (2, core)), False)
+            o_copy(1).wait_recv()
+            project_late(((1, 1 - core),), False)
+            o_copy(2).wait_recv()
+            project_late(((2, 1 - core),), True)
 
         return carry
 

time: 50.3 us -> 50 us (level)
  no operation moved by 1% of the time
where the time goes in v11:
time: 50 us; the launch traced here: 49.9 us
  Pallas kernels  48.9 us (98%)
  local copies, waits for them, and re-layouts  0.97 us (2%)
    pallas_call x1, Pallas kernels, device_step(): pl.pallas_call(functools.partial(kernel, group_size), out_shape=pltpu.VME...  48.9 us

profile of v11, /device:TPU:21, one launch (start us, length us, event | category | flops | bytes accessed | tf_op | source)
XLA Modules:
  0.0 49.9 jit_solution(11330695605594509648)
XLA Ops:
  0.0 48.9 %shard_map.91 = bf16[128,4096]{1,0:T(8,128)(2,1)S(1)} custom-call(bf16[128,4096]{1,0:T(8,128)(2,1)} %x_hbm.1, bf16[4096,4096]{1,0:T(8,128)(2,1)} %wq.1, bf16[4096,1024]{1,0:T(8,128)(2,1)} %wk.1, bf16[4096,1024]{1,0:T(8,128)(2,1)} %wv.1, bf16[4096,4096]{1,0:T(8,128)(2,1)} %wo.1, bf16[32,128]{1,0:T(8,128)(2,1)} %bitcast.3, bf16[1,128]{1,0:T(2,128)(2,1)} %bitcast.4, ...), custom_call_target="tpu_custom_call" | custom-call | tf_op jit(solution)/shard_map/pallas_call | solution.py:520
  48.9 1.0 %copy.11 = bf16[128,4096]{1,0:T(8,128)(2,1)} copy(bf16[128,4096]{1,0:T(8,128)(2,1)S(1)} %shard_map.91) | data formatting | bytes 2097152

commit v12 on v11

--- a/solution.py
+++ b/solution.py
@@ -25,6 +25,7 @@
 SLOTS = len(ORDER)
 EARLY = 2
 FIRST_POLL = 1
+FIRST_DRAIN = 8
 LOW_CHIPS = 2
 LOW_CLOSE = 7
 LOW_OUT = 9
@@ -118,13 +119,11 @@
         for c in range(CORES):
             at, size = span_of(k, c)
             source = pl.ds(c * mixed_dim + stages[k][0] * width, size)
-            copies.append(pltpu.make_async_copy(wo.at[source, :], wo_buf.at[pl.ds(at, size), :], wo_sem.at[k]))
+            copies.append(pltpu.make_async_copy(wo.at[source, :], wo_buf.at[pl.ds(at, size), :], wo_sem))
         return copies
 
-    def wo_wait(k):
-        at, size = span_of(k, 0)
-        span = pl.ds(at, CORES * size)
-        pltpu.make_async_copy(wo.at[span, :], wo_buf.at[span, :], wo_sem.at[k]).wait()
+    def wo_wait():
+        pltpu.make_async_copy(wo, wo_buf, wo_sem).wait()
 
     for copy in small[:1]:
         copy.start()
@@ -167,7 +166,6 @@
                 cols = slice(b * lanes, (b + 1) * lanes)
                 h_buf[core, sl, cols] = (xf[:, cols] * scale * ln_buf[b:b + 1, :].astype(F32)).astype(BF16)
 
-    pl.semaphore_wait(barrier, 1 + 2 * CORES)
     h_copy = pltpu.make_async_remote_copy(h_buf.at[core], h_buf.at[core], h_ssem, h_rsem, device_id={'sp': partner})
 
     def first_copies(idx, e=None):
@@ -201,6 +199,8 @@
             for copy in kv_copies(2):
                 copy.start()
         keep_kv(0, e, raw[:, :head], raw[:, head:])
+        if e == 0:
+            pl.semaphore_wait(barrier, 1 + 2 * CORES)
         for copy, cond in first_copies(0, e):
             pl.when(cond)(copy.start)
     for copy in kv_copies(3):
@@ -400,7 +400,7 @@
 
     def project_early(half):
         if half == 0:
-            wo_wait(0)
+            wo_wait()
             o_copy(0).wait_recv()
         at, size = span_of(0, 0)
         depth = slice(at, at + CORES * size)
@@ -420,6 +420,11 @@
             else:
                 acc[:, cols] = total
 
+    def drain_first(idx, carry):
+        for copy, cond in first_copies(idx):
+            pl.when(cond)(copy.wait_send)
+        return carry
+
     def ring_step(s, carry):
         @pl.when(s >= local_heads)
         def _():
@@ -459,6 +464,8 @@
         def _():
             poll_near(jnp.where(s == FIRST_POLL, local_heads, s + 1))
 
+        pl.when(s == FIRST_DRAIN)(lambda: lax.fori_loop(0, 4, drain_first, None))
+
         for at, late in DEFERRED:
             @pl.when(s + 1 == at)
             def _():
@@ -471,8 +478,6 @@
 
         @pl.when(s == jnp.where(low, LOW_OUT, SLOTS - 1))
         def _():
-            for k in (1, 2):
-                wo_wait(k)
             project_late(((1, core), (2, core)), False)
             o_copy(1).wait_recv()
             project_late(((1, 1 - core),), False)
@@ -486,12 +491,6 @@
     h_copy.wait_send()
     pltpu.make_async_remote_copy(o_send, o_all.at[:, pl.ds(0, mixed_dim)], o_ssem, o_rsem.at[0], device_id={'sp': partner}).wait_send()
 
-    def drain_first(idx, carry):
-        for copy, cond in first_copies(idx):
-            pl.when(cond)(copy.wait_send)
-        return carry
-
-    lax.fori_loop(0, 4, drain_first, 0)
     lax.fori_loop(0, local_heads, drain, 0)
     for dirn in range(2):
         @pl.when(goes_on(dirn, 2))
@@ -542,7 +541,7 @@
                 pltpu.VMEM((head, chip_rows), F32),
                 pltpu.VMEM((rows, head), F32),
                 pltpu.VMEM((rows, head), F32),
-                dma((4,)), dma((4,)), dma((3, 2)), dma((3,)), dma, dma,
+                dma((4,)), dma((4,)), dma((3, 2)), dma, dma, dma,
                 dma((2,)), dma((2,)),
                 dma((2, 4)), dma((2, 2)),
                 dma((2, local_heads + 1)), dma((2, 4 * local_heads)),

time: 50 us -> 49.7 us (level)
  Pallas kernels: 48.9 us -> 48.2 us
    pallas_call x1, Pallas kernels: 48.9 us -> 48.2 us  [device_step(): pl.pallas_call(functools.partial(kernel, group_size), out_shape=pltpu.VME...]
where the time goes in v12:
time: 49.7 us; the launch traced here: 49.2 us
  Pallas kernels  48.2 us (97%)
  local copies, waits for them, and re-layouts  0.97 us (2%)
    pallas_call x1, Pallas kernels, device_step(): pl.pallas_call(functools.partial(kernel, group_size), out_shape=pltpu.VME...  48.2 us

profile of v12, /device:TPU:21, one launch (start us, length us, event | category | flops | bytes accessed | tf_op | source)
XLA Modules:
  0.0 49.2 jit_solution(18167433335218103102)
XLA Ops:
  0.0 48.2 %shard_map.91 = bf16[128,4096]{1,0:T(8,128)(2,1)S(1)} custom-call(bf16[128,4096]{1,0:T(8,128)(2,1)} %x_hbm.1, bf16[4096,4096]{1,0:T(8,128)(2,1)} %wq.1, bf16[4096,1024]{1,0:T(8,128)(2,1)} %wk.1, bf16[4096,1024]{1,0:T(8,128)(2,1)} %wv.1, bf16[4096,4096]{1,0:T(8,128)(2,1)} %wo.1, bf16[32,128]{1,0:T(8,128)(2,1)} %bitcast.3, bf16[1,128]{1,0:T(2,128)(2,1)} %bitcast.4, ...), custom_call_target="tpu_custom_call" | custom-call | tf_op jit(solution)/shard_map/pallas_call | solution.py:519
  48.2 1.0 %copy.11 = bf16[128,4096]{1,0:T(8,128)(2,1)} copy(bf16[128,4096]{1,0:T(8,128)(2,1)S(1)} %shard_map.91) | data formatting | bytes 2097152
